TPU v7x, 128 devices: a whole 4x4x4 slice. The times are simulated.
128 devices in a mesh: gx: 8 (over y, core), gy: 16 (over z, x).
Axes of the slice: x: 4, y: 4, z: 4, core: 2. Of those that a mesh axis runs over, the one named last changes fastest.
Arguments:
- forcing: float32 [16, 512, 2048], P(None, 'gy', 'gx'), may hold values from -6 to 6
- damping: float32 [16, 512, 2048], P(None, 'gy', 'gx'), may hold values from 0.5 to 4
- coupling: float32 [16, 16], replicated, may hold values from -1.5 to 1.5
- wind_lon: float32 [512, 2048], P('gy', 'gx'), may hold values from -0.5 to 0.5
- wind_lat: float32 [512, 2048], P('gy', 'gx'), may hold values from -0.5 to 0.5
Outputs:
- solution: float32 [16, 512, 2048], P(None, 'gy', 'gx')
- residual: float32 [16, 512, 2048], P(None, 'gy', 'gx')
All inputs are finite; a program needn't handle non-finite values.
Results may differ from a plain program's by a relative error of at most 0.0003.
Values sent between devices are 32-bit elements; how exact they have to be, the bound alone decides.
A program may use at most 64 MiB of HBM per device.

v0:
```python
import math

import jax
import jax.numpy as jnp
from jax import lax
from jax.sharding import Mesh
from jax.sharding import PartitionSpec as P

ITERS = 8
GY = ("gy_0", "gy_1")
GX = ("gx_0", "gx_1")
GX_GY = ("gx_0", "gx_1", "gy_0", "gy_1")


COUPLE = 0.25
DIFF_LAT = 0.5
DIFF_LON = 0.5
GUARD = 1.0


def with_halo(cells, sides, width, closed):
    for axis, dim in sides:
        count = lax.axis_size(axis)
        ends = count if closed else count - 1
        head = lax.slice_in_dim(cells, 0, width, axis=dim)
        tail = lax.slice_in_dim(cells, cells.shape[dim] - width, cells.shape[dim], axis=dim)
        cells = jnp.concatenate(
            [
                lax.ppermute(tail, axis, [(i, (i + 1) % count) for i in range(ends)]),
                cells,
                lax.ppermute(head, axis, [((i + 1) % count, i) for i in range(ends)]),
            ],
            axis=dim,
        )
    return cells


def one_axis_at_a_time(value, axes):
    for axis in axes:
        value = lax.psum(value, axis)
    return value


def apply_core(padded, damping, coupling, wind_lon, wind_lat, diffuse_lon):
    centre = padded[:, 2:-2, 2:-2]
    east_one = padded[:, 2:-2, 3:-1]
    west_one = padded[:, 2:-2, 1:-3]
    east_two = padded[:, 2:-2, 4:]
    west_two = padded[:, 2:-2, :-4]
    north_one = padded[:, 3:-1, 2:-2]
    south_one = padded[:, 1:-3, 2:-2]
    north_two = padded[:, 4:, 2:-2]
    south_two = padded[:, :-4, 2:-2]
    slope_lon = (8.0 * (east_one - west_one) - (east_two - west_two)) / 12.0
    slope_lat = (8.0 * (north_one - south_one) - (north_two - south_two)) / 12.0
    coupled = COUPLE * jnp.einsum("ij,jab->iab", coupling, centre, precision=lax.Precision.HIGHEST)
    return (
        (1.0 + damping) * centre
        + coupled
        + diffuse_lon * (2.0 * centre - east_one - west_one)
        + DIFF_LAT * (2.0 * centre - north_one - south_one)
        + wind_lon * slope_lon
        + wind_lat * slope_lat
    )


def lon_diffusion(row_pos, lat_total):
    phi = -math.pi / 2 + (row_pos + 0.5) * (math.pi / lat_total)
    return DIFF_LON / (jnp.cos(phi) ** 2 + 0.1)


def crop_rim(source, rim_have, rim_want):
    margin = rim_have - rim_want
    if margin == 0:
        return source
    return source[:, margin : source.shape[1] - margin, margin : source.shape[2] - margin]


def least_squares(heights, first):
    num_steps = heights.shape[1]
    target = jnp.zeros((num_steps + 1,), jnp.float32).at[0].set(first)
    rotated = heights
    cosines = []
    sines = []
    for column in range(num_steps):
        column_vec = rotated[:, column]
        for earlier in range(column):
            upper_val = column_vec[earlier]
            lower_val = column_vec[earlier + 1]
            column_vec = column_vec.at[earlier].set(
                cosines[earlier] * upper_val + sines[earlier] * lower_val
            )
            column_vec = column_vec.at[earlier + 1].set(
                -sines[earlier] * upper_val + cosines[earlier] * lower_val
            )
        upper_val = column_vec[column]
        lower_val = column_vec[column + 1]
        radius = jnp.sqrt(upper_val * upper_val + lower_val * lower_val)
        cosine = upper_val / radius
        sine_val = lower_val / radius
        column_vec = column_vec.at[column].set(radius).at[column + 1].set(0.0)
        rotated = rotated.at[:, column].set(column_vec)
        upper_val = target[column]
        lower_val = target[column + 1]
        target = target.at[column].set(cosine * upper_val + sine_val * lower_val)
        target = target.at[column + 1].set(-sine_val * upper_val + cosine * lower_val)
        cosines.append(cosine)
        sines.append(sine_val)
    weights = [None] * num_steps
    for column in reversed(range(num_steps)):
        partial_value = target[column]
        for later_col in range(column + 1, num_steps):
            partial_value = partial_value - rotated[column, later_col] * weights[later_col]
        weights[column] = partial_value / rotated[column, column]
    return weights


def per_device(forcing, damping, coupling, wind_lon, wind_lat):
    channels, lat_rows, lon_cols = forcing.shape
    lat_total = lat_rows * lax.axis_size(GY)
    extent = 2 * ITERS
    stacked = jnp.concatenate([forcing, damping, wind_lon[None], wind_lat[None]], axis=0)
    stacked = with_halo(stacked, ((GX, 2),), extent, True)
    stacked = with_halo(stacked, ((GY, 1),), extent, False)
    row_pos = (lax.axis_index(GY) * lat_rows - extent + jnp.arange(lat_rows + 2 * extent)).astype(
        jnp.float32
    )
    full_shape = (1, lat_rows + 2 * extent, lon_cols + 2 * extent)
    inside = ((row_pos >= 0.0) & (row_pos < lat_total)).astype(jnp.float32)
    inside_full = jnp.broadcast_to(inside[None, :, None], full_shape)
    diffuse_full = jnp.broadcast_to(lon_diffusion(row_pos, lat_total)[None, :, None], full_shape)
    damp_ext = stacked[channels : 2 * channels]
    zonal_ext = stacked[2 * channels : 2 * channels + 1]
    merid_ext = stacked[2 * channels + 1 :]

    def matvec(source, rim_in):
        rim_out = rim_in - 2
        result = apply_core(
            source,
            crop_rim(damp_ext, extent, rim_out),
            coupling,
            crop_rim(zonal_ext, extent, rim_out),
            crop_rim(merid_ext, extent, rim_out),
            crop_rim(diffuse_full, extent, rim_out),
        )
        return (result * crop_rim(inside_full, extent, rim_out), rim_out)

    initial = (stacked[:channels], extent)
    interior = crop_rim(initial[0], initial[1], 0)
    total_sq = one_axis_at_a_time(jnp.sum(interior * interior), GX_GY)
    scale_first = jnp.sqrt(total_sq + GUARD)
    krylov = [(initial[0] / scale_first, initial[1])]
    heights = jnp.zeros((ITERS + 1, ITERS), jnp.float32)
    gram = (
        jnp.zeros((ITERS, ITERS), jnp.float32).at[0, 0].set(total_sq / (scale_first * scale_first))
    )
    for column in range(ITERS):
        applied, rim_new = matvec(krylov[column][0], krylov[column][1])
        applied_in = crop_rim(applied, rim_new, 0)
        local_dots = jnp.stack(
            [jnp.sum(crop_rim(vector, rim_vec, 0) * applied_in) for vector, rim_vec in krylov]
        )
        count = len(krylov)
        coeffs, squared = (
            one_axis_at_a_time(local_dots, GX_GY),
            one_axis_at_a_time(jnp.sum(applied_in * applied_in), GX_GY),
        )
        for earlier in range(count):
            applied = applied - coeffs[earlier] * crop_rim(
                krylov[earlier][0], krylov[earlier][1], rim_new
            )
        gram_now = gram[:count, :count]
        gram_coef = jnp.sum(gram_now * coeffs[None, :], axis=1)
        norm_sq = jnp.maximum(
            squared - 2.0 * jnp.sum(coeffs * coeffs) + jnp.sum(coeffs * gram_coef), 0.0
        )
        subdiag = jnp.sqrt(norm_sq + GUARD)
        if column + 1 < ITERS:
            cross = (coeffs - gram_coef) / subdiag
            gram = gram.at[count, :count].set(cross).at[:count, count].set(cross)
            gram = gram.at[count, count].set(norm_sq / (subdiag * subdiag))
        heights = heights.at[: column + 1, column].set(coeffs).at[column + 1, column].set(subdiag)
        if column + 1 < ITERS:
            krylov.append((applied / subdiag, rim_new))
    weights = least_squares(heights, scale_first)
    rim_last = krylov[-1][1]
    solution = weights[0] * crop_rim(krylov[0][0], krylov[0][1], rim_last)
    for column in range(1, ITERS):
        solution = solution + weights[column] * crop_rim(
            krylov[column][0], krylov[column][1], rim_last
        )
    applied, rim_done = matvec(solution, rim_last)
    residual = interior - crop_rim(applied, rim_done, 0)
    return (crop_rim(solution, rim_last, 0), residual)


def solution(mesh):
    finer = Mesh(mesh.devices.reshape(4, 2, 4, 4), ("gx_0", "gx_1", "gy_0", "gy_1"))
    in_specs = (P(None, GY, GX), P(None, GY, GX), P(), P(GY, GX), P(GY, GX))
    out_specs = (P(None, GY, GX), P(None, GY, GX))
    return jax.shard_map(
        per_device, mesh=finer, in_specs=in_specs, out_specs=out_specs, check_vma=False
    )
```

profile of v0, /device:TPU:0, one launch (start us, length us, event | category | flops | bytes accessed | tf_op | source)
XLA Modules:
  0.0 691.3 jit_solution(11253868314345148001)
XLA Ops:
  13.4 9.4 %psum.476 = f32[]{:T(128)} all-reduce(f32[]{:T(128)} %multiply_reduce_fusion.44), channel_id=1, replica_groups=mesh['gx_0'=4,'gx_1'=2,'gy_0'=4,'gy_1'=4] {'gx_0'}, use_global_device_ids=true, to_apply=%region_1.0 | all-reduce | flops 1 | bytes 8 | tf_op jit(solution)/shard_map/psum | solution.py:40
  27.3 12.4 %psum.478 = f32[]{:T(128)} all-reduce(f32[]{:T(128)} %psum.477), channel_id=1, replica_groups=mesh['gx_0'=4,'gx_1'=2,'gy_0'=4,'gy_1'=4] {'gy_0'}, use_global_device_ids=true, to_apply=%region_3.0 | all-reduce | flops 1 | bytes 8 | tf_op jit(solution)/shard_map/psum | solution.py:40
  40.4 11.1 %psum.479 = f32[]{:T(128)} all-reduce(f32[]{:T(128)} %psum.478), channel_id=1, replica_groups=mesh['gx_0'=4,'gx_1'=2,'gy_0'=4,'gy_1'=4] {'gy_1'}, use_global_device_ids=true, to_apply=%region_4.0 | all-reduce | flops 1 | bytes 8 | tf_op jit(solution)/shard_map/psum | solution.py:40
  67.4 4.6 collective-permute-start.2
  72.1 12.4 %collective-permute-done.3 = f32[34,16,288]{2,1,0:T(8,128)S(1)} collective-permute-done((f32[34,16,288]{2,1,0:T(8,128)S(1)}, f32[34,16,288]{2,1,0:T(8,128)S(1)}, u32[]{:S(2)}, u32[]{:S(2)}) %collective-permute-start.3) | collective-permute-done | bytes 626720 | tf_op jit(solution)/shard_map/ppermute | solution.py:31
  86.2 5.5 pad_maximum_fusion
  93.5 4.6 fusion.3
  99.2 9.3 %all-reduce.26 = (f32[]{:T(128)}, f32[1]{0:T(128)}) all-reduce(f32[]{:T(128)} %get-tuple-element.1627, f32[1]{0:T(128)} %bitcast.5), channel_id=1, replica_groups=mesh['gx_0'=4,'gx_1'=2,'gy_0'=4,'gy_1'=4] {'gx_0'}, use_global_device_ids=true, to_apply=%region_11.0 | all-reduce | flops 2 | bytes 16 | tf_op jit(solution)/shard_map/psum | solution.py:40
  111.6 12.4 %all-reduce.18 = (f32[]{:T(128)}, f32[1]{0:T(128)}) all-reduce(f32[]{:T(128)} %get-tuple-element.1746, f32[1]{0:T(128)} %get-tuple-element.1747), channel_id=1, replica_groups=mesh['gx_0'=4,'gx_1'=2,'gy_0'=4,'gy_1'=4] {'gy_0'}, use_global_device_ids=true, to_apply=%region_13.0 | all-reduce | flops 2 | bytes 16 | tf_op jit(solution)/shard_map/psum | solution.py:40
  124.1 8.6 %all-reduce.10 = (f32[]{:T(128)}, f32[1]{0:T(128)}) all-reduce(f32[]{:T(128)} %get-tuple-element.1714, f32[1]{0:T(128)} %get-tuple-element.1715), channel_id=1, replica_groups=mesh['gx_0'=4,'gx_1'=2,'gy_0'=4,'gy_1'=4] {'gy_1'}, use_global_device_ids=true, to_apply=%region_14.0 | all-reduce | flops 2 | bytes 16 | tf_op jit(solution)/shard_map/psum | solution.py:40
  140.9 5.4 fusion.21
  154.7 9.5 %all-reduce.25 = (f32[]{:T(128)}, f32[2]{0:T(128)S(1)}) all-reduce(f32[]{:T(128)} %get-tuple-element.1630, f32[2]{0:T(128)S(1)} %pad_maximum_fusion.3), channel_id=1, replica_groups=mesh['gx_0'=4,'gx_1'=2,'gy_0'=4,'gy_1'=4] {'gx_0'}, use_global_device_ids=true, to_apply=%region_23.0 | all-reduce | flops 3 | bytes 24 | tf_op jit(solution)/shard_map/psum | solution.py:40
  167.3 8.8 %all-reduce.17 = (f32[]{:T(128)}, f32[2]{0:T(128)S(1)}) all-reduce(f32[]{:T(128)} %get-tuple-element.1744, f32[2]{0:T(128)S(1)} %get-tuple-element.1745), channel_id=1, replica_groups=mesh['gx_0'=4,'gx_1'=2,'gy_0'=4,'gy_1'=4] {'gy_0'}, use_global_device_ids=true, to_apply=%region_25.0 | all-reduce | flops 3 | bytes 24 | tf_op jit(solution)/shard_map/psum | solution.py:40
  176.0 10.0 %all-reduce.9 = (f32[]{:T(128)}, f32[2]{0:T(128)S(1)}) all-reduce(f32[]{:T(128)} %get-tuple-element.1712, f32[2]{0:T(128)S(1)} %get-tuple-element.1713), channel_id=1, replica_groups=mesh['gx_0'=4,'gx_1'=2,'gy_0'=4,'gy_1'=4] {'gy_1'}, use_global_device_ids=true, to_apply=%region_26.0 | all-reduce | flops 3 | bytes 24 | tf_op jit(solution)/shard_map/psum | solution.py:40
  194.4 5.6 fusion.39
  206.9 9.2 %all-reduce.24 = (f32[]{:T(128)}, f32[3]{0:T(128)S(1)}) all-reduce(f32[]{:T(128)} %get-tuple-element.1634, f32[3]{0:T(128)S(1)} %pad_maximum_fusion.4), channel_id=1, replica_groups=mesh['gx_0'=4,'gx_1'=2,'gy_0'=4,'gy_1'=4] {'gx_0'}, use_global_device_ids=true, to_apply=%region_39.0 | all-reduce | flops 4 | bytes 32 | tf_op jit(solution)/shard_map/psum | solution.py:40
  219.2 10.4 %all-reduce.16 = (f32[]{:T(128)}, f32[3]{0:T(128)S(1)}) all-reduce(f32[]{:T(128)} %get-tuple-element.1742, f32[3]{0:T(128)S(1)} %get-tuple-element.1743), channel_id=1, replica_groups=mesh['gx_0'=4,'gx_1'=2,'gy_0'=4,'gy_1'=4] {'gy_0'}, use_global_device_ids=true, to_apply=%region_41.0 | all-reduce | flops 4 | bytes 32 | tf_op jit(solution)/shard_map/psum | solution.py:40
  229.6 8.3 %all-reduce.8 = (f32[]{:T(128)}, f32[3]{0:T(128)S(1)}) all-reduce(f32[]{:T(128)} %get-tuple-element.1710, f32[3]{0:T(128)S(1)} %get-tuple-element.1711), channel_id=1, replica_groups=mesh['gx_0'=4,'gx_1'=2,'gy_0'=4,'gy_1'=4] {'gy_1'}, use_global_device_ids=true, to_apply=%region_42.0 | all-reduce | flops 4 | bytes 32 | tf_op jit(solution)/shard_map/psum | solution.py:40
  243.3 4.7 fusion.34
  248.0 5.2 fusion.73
  262.5 9.6 %all-reduce.23 = (f32[]{:T(128)}, f32[4]{0:T(128)S(1)}) all-reduce(f32[]{:T(128)} %get-tuple-element.1639, f32[4]{0:T(128)S(1)} %pad_maximum_fusion.5), channel_id=1, replica_groups=mesh['gx_0'=4,'gx_1'=2,'gy_0'=4,'gy_1'=4] {'gx_0'}, use_global_device_ids=true, to_apply=%region_56.0 | all-reduce | flops 5 | bytes 40 | tf_op jit(solution)/shard_map/psum | solution.py:40
  275.2 8.8 %all-reduce.15 = (f32[]{:T(128)}, f32[4]{0:T(128)S(1)}) all-reduce(f32[]{:T(128)} %get-tuple-element.1740, f32[4]{0:T(128)S(1)} %get-tuple-element.1741), channel_id=1, replica_groups=mesh['gx_0'=4,'gx_1'=2,'gy_0'=4,'gy_1'=4] {'gy_0'}, use_global_device_ids=true, to_apply=%region_58.0 | all-reduce | flops 5 | bytes 40 | tf_op jit(solution)/shard_map/psum | solution.py:40
  284.1 10.0 %all-reduce.7 = (f32[]{:T(128)}, f32[4]{0:T(128)S(1)}) all-reduce(f32[]{:T(128)} %get-tuple-element.1708, f32[4]{0:T(128)S(1)} %get-tuple-element.1709), channel_id=1, replica_groups=mesh['gx_0'=4,'gx_1'=2,'gy_0'=4,'gy_1'=4] {'gy_1'}, use_global_device_ids=true, to_apply=%region_59.0 | all-reduce | flops 5 | bytes 40 | tf_op jit(solution)/shard_map/psum | solution.py:40
  299.0 5.8 fusion.67
  304.8 4.9 fusion.93
  320.0 9.3 %all-reduce.22 = (f32[]{:T(128)}, f32[5]{0:T(128)S(1)}) all-reduce(f32[]{:T(128)} %get-tuple-element.1644, f32[5]{0:T(128)S(1)} %stack.147), channel_id=1, replica_groups=mesh['gx_0'=4,'gx_1'=2,'gy_0'=4,'gy_1'=4] {'gx_0'}, use_global_device_ids=true, to_apply=%region_74.0 | all-reduce | flops 6 | bytes 48 | tf_op jit(solution)/shard_map/psum | solution.py:40
  332.4 10.4 %all-reduce.14 = (f32[]{:T(128)}, f32[5]{0:T(128)S(1)}) all-reduce(f32[]{:T(128)} %get-tuple-element.1738, f32[5]{0:T(128)S(1)} %get-tuple-element.1739), channel_id=1, replica_groups=mesh['gx_0'=4,'gx_1'=2,'gy_0'=4,'gy_1'=4] {'gy_0'}, use_global_device_ids=true, to_apply=%region_76.0 | all-reduce | flops 6 | bytes 48 | tf_op jit(solution)/shard_map/psum | solution.py:40
  342.8 8.3 %all-reduce.6 = (f32[]{:T(128)}, f32[5]{0:T(128)S(1)}) all-reduce(f32[]{:T(128)} %get-tuple-element.1706, f32[5]{0:T(128)S(1)} %get-tuple-element.1707), channel_id=1, replica_groups=mesh['gx_0'=4,'gx_1'=2,'gy_0'=4,'gy_1'=4] {'gy_1'}, use_global_device_ids=true, to_apply=%region_77.0 | all-reduce | flops 6 | bytes 48 | tf_op jit(solution)/shard_map/psum | solution.py:40
  356.2 6.8 fusion.86
  363.1 4.5 fusion.114
  374.9 3.8 stack.154
  378.7 9.5 %all-reduce.21 = (f32[]{:T(128)}, f32[6]{0:T(128)S(1)}) all-reduce(f32[]{:T(128)} %get-tuple-element.1651, f32[6]{0:T(128)S(1)} %stack.154), channel_id=1, replica_groups=mesh['gx_0'=4,'gx_1'=2,'gy_0'=4,'gy_1'=4] {'gx_0'}, use_global_device_ids=true, to_apply=%region_93.0 | all-reduce | flops 7 | bytes 56 | tf_op jit(solution)/shard_map/psum | solution.py:40
  391.3 8.8 %all-reduce.13 = (f32[]{:T(128)}, f32[6]{0:T(128)S(1)}) all-reduce(f32[]{:T(128)} %get-tuple-element.1736, f32[6]{0:T(128)S(1)} %get-tuple-element.1737), channel_id=1, replica_groups=mesh['gx_0'=4,'gx_1'=2,'gy_0'=4,'gy_1'=4] {'gy_0'}, use_global_device_ids=true, to_apply=%region_95.0 | all-reduce | flops 7 | bytes 56 | tf_op jit(solution)/shard_map/psum | solution.py:40
  400.1 10.0 %all-reduce.5 = (f32[]{:T(128)}, f32[6]{0:T(128)S(1)}) all-reduce(f32[]{:T(128)} %get-tuple-element.1704, f32[6]{0:T(128)S(1)} %get-tuple-element.1705), channel_id=1, replica_groups=mesh['gx_0'=4,'gx_1'=2,'gy_0'=4,'gy_1'=4] {'gy_1'}, use_global_device_ids=true, to_apply=%region_96.0 | all-reduce | flops 7 | bytes 56 | tf_op jit(solution)/shard_map/psum | solution.py:40
  414.1 7.7 %fusion.106 = f32[16,40,264]{2,0,1:T(8,128)S(1)} fusion(f32[16,48,272]{2,0,1:T(8,128)} %copy-done.3, f32[16,52,276]{2,0,1:T(8,128)} %copy-done.2, f32[16,56,280]{2,0,1:T(8,128)} %copy-done.1, f32[16,60,284]{2,0,1:T(8,128)S(1)} %subtract_divide_fusion, f32[16,40,264]{2,0,1:T(8,128)} %copy-done.16, f32[16,64,288]{2,0,1:T(8,128)S(1)} %slice_divide_fusion, ...), kind=kLoop, calls=%fused_computation.139 | loop fusion | flops 2196480 | bytes 5406748 | tf_op jit(solution)/shard_map/div | solution.py:184
  421.8 4.2 fusion.128
  426.1 4.1 multiply_reduce_fusion.10
  433.9 4.5 stack.162
  438.4 9.2 %all-reduce.20 = (f32[]{:T(128)}, f32[7]{0:T(128)S(1)}) all-reduce(f32[]{:T(128)} %get-tuple-element.1659, f32[7]{0:T(128)S(1)} %stack.162), channel_id=1, replica_groups=mesh['gx_0'=4,'gx_1'=2,'gy_0'=4,'gy_1'=4] {'gx_0'}, use_global_device_ids=true, to_apply=%region_113.0 | all-reduce | flops 8 | bytes 64 | tf_op jit(solution)/shard_map/psum | solution.py:40
  450.7 10.3 %all-reduce.12 = (f32[]{:T(128)}, f32[7]{0:T(128)S(1)}) all-reduce(f32[]{:T(128)} %get-tuple-element.1734, f32[7]{0:T(128)S(1)} %get-tuple-element.1735), channel_id=1, replica_groups=mesh['gx_0'=4,'gx_1'=2,'gy_0'=4,'gy_1'=4] {'gy_0'}, use_global_device_ids=true, to_apply=%region_115.0 | all-reduce | flops 8 | bytes 64 | tf_op jit(solution)/shard_map/psum | solution.py:40
  461.1 8.3 %all-reduce.4 = (f32[]{:T(128)}, f32[7]{0:T(128)S(1)}) all-reduce(f32[]{:T(128)} %get-tuple-element.1702, f32[7]{0:T(128)S(1)} %get-tuple-element.1703), channel_id=1, replica_groups=mesh['gx_0'=4,'gx_1'=2,'gy_0'=4,'gy_1'=4] {'gy_1'}, use_global_device_ids=true, to_apply=%region_116.0 | all-reduce | flops 8 | bytes 64 | tf_op jit(solution)/shard_map/psum | solution.py:40
  494.3 8.8 %subtract_divide_fusion.1 = f32[16,36,260]{2,0,1:T(8,128)S(1)} fusion(f32[16,36,260]{2,0,1:T(8,128)} %copy-done.17, f32[16,44,268]{2,0,1:T(8,128)} %copy-done.4, f32[16,48,272]{2,0,1:T(8,128)} %copy-done.3, f32[16,52,276]{2,0,1:T(8,128)} %copy-done.2, f32[16,56,280]{2,0,1:T(8,128)} %copy-done.1, f32[16,60,284]{2,0,1:T(8,128)S(1)} %subtract_divide_fusion, ...), kind=kLoop, calls=%fused_computation.178 | loop fusion | flops 2246400 | bytes 5391392 | tf_op jit(solution)/shard_map/div | solution.py:184
  503.1 5.2 multiply_reduce_fusion
  508.3 5.1 stack.171
  513.3 9.4 %all-reduce.19 = (f32[8]{0:T(128)S(1)}, f32[]{:T(128)}) all-reduce(f32[8]{0:T(128)S(1)} %stack.171, f32[]{:T(128)} %get-tuple-element.1661), channel_id=1, replica_groups=mesh['gx_0'=4,'gx_1'=2,'gy_0'=4,'gy_1'=4] {'gx_0'}, use_global_device_ids=true, to_apply=%region_129.0 | all-reduce | flops 9 | bytes 72 | tf_op jit(solution)/shard_map/psum | solution.py:40
  525.8 8.8 %all-reduce.11 = (f32[8]{0:T(128)S(1)}, f32[]{:T(128)}) all-reduce(f32[8]{0:T(128)S(1)} %get-tuple-element.1732, f32[]{:T(128)} %get-tuple-element.1733), channel_id=1, replica_groups=mesh['gx_0'=4,'gx_1'=2,'gy_0'=4,'gy_1'=4] {'gy_0'}, use_global_device_ids=true, to_apply=%region_131.0 | all-reduce | flops 9 | bytes 72 | tf_op jit(solution)/shard_map/psum | solution.py:40
  534.7 9.9 %all-reduce.3 = (f32[8]{0:T(128)S(1)}, f32[]{:T(128)}) all-reduce(f32[8]{0:T(128)S(1)} %get-tuple-element.1700, f32[]{:T(128)} %get-tuple-element.1701), channel_id=1, replica_groups=mesh['gx_0'=4,'gx_1'=2,'gy_0'=4,'gy_1'=4] {'gy_1'}, use_global_device_ids=true, to_apply=%region_132.0 | all-reduce | flops 9 | bytes 72 | tf_op jit(solution)/shard_map/psum | solution.py:40
  682.0 4.3 multiply_add_fusion
  (386 shorter events, 197.1 us)
Async XLA Ops:
  0.6 92.9 %copy-start = (f32[16,16]{1,0:T(8,128)S(1)}, f32[16,16]{1,0:T(8,128)}, u32[]{:S(2)}) copy-start(f32[16,16]{1,0:T(8,128)} %param.277) | copy-start | bytes 3076
  0.6 3.0 copy-start.18
  5.1 4.3 copy-start.19
  5.1 48.3 %copy-start.30 = (s32[2]{0:T(128)S(1)}, s32[2]{0:T(128)}, u32[]{:S(2)}) copy-start(s32[2]{0:T(128)} %constant.2816.clone.1) | copy-start | bytes 28
  5.1 49.7 %copy-start.29 = (s32[2]{0:T(128)S(1)}, s32[2]{0:T(128)}, u32[]{:S(2)}) copy-start(s32[2]{0:T(128)} %constant.2818.clone.1) | copy-start | bytes 28
  5.1 51.0 %copy-start.28 = (s32[2]{0:T(128)S(1)}, s32[2]{0:T(128)}, u32[]{:S(2)}) copy-start(s32[2]{0:T(128)} %constant.2819.clone.1) | copy-start | bytes 28
  5.1 52.2 %copy-start.27 = (s32[2]{0:T(128)S(1)}, s32[2]{0:T(128)}, u32[]{:S(2)}) copy-start(s32[2]{0:T(128)} %constant.2821.clone.1) | copy-start | bytes 28
  5.1 53.4 %copy-start.26 = (s32[2]{0:T(128)S(1)}, s32[2]{0:T(128)}, u32[]{:S(2)}) copy-start(s32[2]{0:T(128)} %constant.2823.clone.1) | copy-start | bytes 28
  5.2 54.7 %copy-start.25 = (s32[2]{0:T(128)S(1)}, s32[2]{0:T(128)}, u32[]{:S(2)}) copy-start(s32[2]{0:T(128)} %constant.2824.clone.1) | copy-start | bytes 28
  6.6 54.5 %collective-permute-start.1 = (f32[34,32,16]{0,2,1:T(8,128)S(1)}, f32[34,32,16]{0,2,1:T(8,128)S(1)}, u32[]{:S(2)}, u32[]{:S(2)}) collective-permute-start(f32[34,32,16]{0,2,1:T(8,128)S(1)} %copy.22), channel_id=1, source_target_pairs={{16,0},{32,16},{48,32},{64,48},{80,64},{96,80},{112,96},{0,112},{1... | collective-permute-start | bytes 208904 | tf_op jit(solution)/shard_map/ppermute | solution.py:31
  9.4 52.8 %collective-permute-start = (f32[34,32,16]{0,2,1:T(8,128)S(1)}, f32[34,32,16]{0,2,1:T(8,128)S(1)}, u32[]{:S(2)}, u32[]{:S(2)}) collective-permute-start(f32[34,32,16]{0,2,1:T(8,128)S(1)} %copy.21), channel_id=1, source_target_pairs={{0,16},{16,32},{32,48},{48,64},{64,80},{80,96},{96,112},{112,0},{1... | collective-permute-start | bytes 208904 | tf_op jit(solution)/shard_map/ppermute | solution.py:29
  65.9 6.3 copy-start.23
  65.9 6.2 copy-start.24
  65.9 18.6 %collective-permute-start.3 = (f32[34,16,288]{2,1,0:T(8,128)S(1)}, f32[34,16,288]{2,1,0:T(8,128)S(1)}, u32[]{:S(2)}, u32[]{:S(2)}) collective-permute-start(f32[34,16,288]{2,1,0:T(8,128)S(1)} %copy.26), channel_id=1, source_target_pairs={{1,0},{2,1},{3,2},{4,3},{5,4},{6,5},{7,6},{8,7},{9,8},{10,9},{11,1... | collective-permute-start | bytes 1880072 | tf_op jit(solution)/shard_map/ppermute | solution.py:31
  67.4 18.5 %collective-permute-start.2 = (f32[34,16,288]{2,1,0:T(8,128)S(1)}, f32[34,16,288]{2,1,0:T(8,128)S(1)}, u32[]{:S(2)}, u32[]{:S(2)}) collective-permute-start(f32[34,16,288]{2,1,0:T(8,128)S(1)} %copy.25), channel_id=1, source_target_pairs={{0,1},{1,2},{2,3},{3,4},{4,5},{5,6},{6,7},{7,8},{8,9},{9,10},{10,1... | collective-permute-start | bytes 1880072 | tf_op jit(solution)/shard_map/ppermute | solution.py:29
  84.8 1.4 copy-start.8
  84.8 1.4 copy-start.9
  91.7 1.9 copy-start.7
  98.2 40.2 %copy-start.11 = (f32[16,60,284]{2,0,1:T(8,128)}, f32[16,60,284]{2,0,1:T(8,128)S(1)}, u32[]{:S(2)}) copy-start(f32[16,60,284]{2,0,1:T(8,128)S(1)} %fusion.3) | copy-start | bytes 3271684
  146.4 1.1 copy-start.12
  194.3 5.6 copy-start.1
  199.9 1.3 copy-start.13
  248.0 5.2 copy-start.2
  253.2 3.0 copy-start.14
  304.8 4.9 copy-start.3
  309.8 3.4 copy-start.15
  363.0 4.5 copy-start.4
  367.6 3.7 copy-start.16
  421.8 4.2 copy-start.5
  426.1 4.1 copy-start.17
  494.3 8.8 %copy-start.6 = (f32[16,40,264]{2,0,1:T(8,128)S(1)}, f32[16,40,264]{2,0,1:T(8,128)}, u32[]{:S(2)}) copy-start(f32[16,40,264]{2,0,1:T(8,128)} %copy-done.5) | copy-start | bytes 2027524
  494.3 8.8 %copy-start.21 = (f32[16,32,256]{2,1,0:T(8,128)S(1)}, f32[16,32,256]{2,1,0:T(8,128)}, u32[]{:S(2)}) copy-start(f32[16,32,256]{2,1,0:T(8,128)} %param.276) | copy-start | bytes 1572868
  503.1 5.2 copy-start.10
  682.0 4.5 copy-start.20
  682.0 4.5 copy-start.22
where the time goes:
time: 704 us; the launch traced here: 691 us
  blocking collectives  288 us (41%)
  other arithmetic  128 us (18%)
  between operations  117 us (17%)
  local copies, waits for them, and re-layouts  94.7 us (13%)
  matrix products  41.7 us (6%)
  waiting for transfers between devices  13.4 us (2%)
  starting transfers between devices  8.48 us (1%)
    psum x36, blocking collectives, one_axis_at_a_time(): value = lax.psum(value, axis)  288 us
    dot_general x9, matrix products, apply_core(): jnp.einsum('ij,jab->iab', coupling, centre, precision=lax.Precision.HIGHEST)  41.7 us
    div x7, other arithmetic, per_device(): krylov.append((applied / subdiag, rim_new))  39.6 us
    another operation x38, other arithmetic  38.6 us
    reduce_sum x7, other arithmetic, per_device(): jnp.sum(crop_rim(vector, rim_vec, 0) * applied_in)  17.7 us
    another operation x4, local copies, waits for them, and re-layouts, per_device(): jnp.stack([jnp.sum(crop_rim(vector, rim_vec, 0) * applied_in) for vector,...  16.5 us
    slice x25, local copies, waits for them, and re-layouts, least_squares(): lower_val = column_vec[earlier + 1]  15.2 us
  transfers between devices with their start and end apart: 4, of which 2 were waited for; matrix products, arithmetic and copies ran while one was open for 2% of the time, Pallas kernels for 0%

commit v1 on v0

v1 whole, which is shorter than its diff:
```python
import functools
import math

import jax
import jax.numpy as jnp
import numpy as np
from jax import lax
from jax.experimental import pallas as pl
from jax.experimental.pallas import tpu as pltpu
from jax.sharding import PartitionSpec as P

ITERS = 8
CH = 16
RIM = 8
LOW, HIGH = 1.0, 16.0
MID, HALF = (LOW + HIGH) / 2, (HIGH - LOW) / 2
BLOCK = 4
NOISE = 1.2e-7
TRUST = 1.0e-4
MESH = pl.DeviceIdType.MESH
F32 = jnp.float32


def trial_table():
    rng = np.random.default_rng(7)
    draw = rng.choice([-1.0, 1.0], size=(9, 16, 128)) * NOISE
    table = np.zeros((9, 16, 128), np.float32)
    for i in range(9):
        for k in range(i, 9):
            table[i, k] = draw[i, k]
            table[k, i] = draw[i, k]
    table[:, :, 0] = 0.0
    return table


def kx_table(lat_total):
    row = np.arange(lat_total) + 0.5
    phi = -math.pi / 2 + row * (math.pi / lat_total)
    table = np.zeros((lat_total + 2 * RIM, 128), np.float32)
    table[RIM : RIM + lat_total] = (0.5 / (np.cos(phi) ** 2 + 0.1))[:, None]
    return table


def lanes(shape):
    return lax.broadcasted_iota(jnp.int32, shape, len(shape) - 1)


def apply_a(vec):
    sub = lax.broadcasted_iota(jnp.int32, vec.shape, 0)
    up = pltpu.roll(vec, 1, 0)
    kept = jnp.where((sub == 0) | (sub == BLOCK), 0.0, vec)
    down = pltpu.roll(kept, 15, 0)
    return MID * vec + (HALF / 2) * (up + down)


def mat_vec(cols, vec, count):
    total = cols[0] * vec[0:1, :]
    for k in range(1, count):
        total = total + cols[k] * vec[k : k + 1, :]
    return total


def dot(a, b):
    return jnp.sum(a * b, axis=0, keepdims=True)


def gmres(cols):
    sub = lax.broadcasted_iota(jnp.int32, (16, 128), 0)
    first = jnp.sqrt(cols[0][0:1, :] + 1.0)
    basis = [jnp.where(sub == 0, 1.0, 0.0) / first]
    target = first
    targets = []
    columns = []
    turns = []
    for j in range(ITERS):
        w = apply_a(basis[j])
        u = mat_vec(cols, w, j + 2)
        h = [dot(v, u) for v in basis]
        for i in range(j + 1):
            w = w - h[i] * basis[i]
        norm = dot(w, mat_vec(cols, w, j + 2))
        below = jnp.sqrt(jnp.maximum(norm, 0.0) + 1.0)
        if j + 1 < ITERS:
            basis.append(w / below)
        col = list(h)
        for i, (c, s) in enumerate(turns):
            if i + 1 <= j:
                col[i], col[i + 1] = c * col[i] + s * col[i + 1], c * col[i + 1] - s * col[i]
        radius = jnp.sqrt(col[j] * col[j] + below * below)
        inv = 1.0 / radius
        c, s = col[j] * inv, below * inv
        turns.append((c, s))
        col[j] = radius
        columns.append((col, inv))
        targets.append(c * target)
        target = -s * target
    y = [None] * ITERS
    for j in reversed(range(ITERS)):
        y[j] = targets[j] * columns[j][1]
        for i in range(j):
            targets[i] = targets[i] - columns[j][0][i] * y[j]
    q = basis[0] * y[0]
    for j in range(1, ITERS):
        q = q + basis[j] * y[j]
    return q


def kernel(
    nx, ny, stk, coup, trial, kxs, sol, res, flag,
    ext, pwr, coef, lon, pack, kxv, gx_slots, gy_slots,
    in_sem, kx_sem, lon_send, lon_recv, lat_send, lat_recv, cor_send, cor_recv,
    mid_send, mid_recv, gxs_send, gxs_recv, gys_send, gys_recv,
):
    gx, gy = lax.axis_index("gx"), lax.axis_index("gy")
    rows = stk.shape[0]
    top = RIM + rows
    total = rows + 2 * RIM
    east, west = lax.rem(gx + 1, nx), lax.rem(gx + nx - 1, nx)
    north, south = gy + 1, gy - 1
    has_n, has_s = gy < ny - 1, gy > 0

    own = pltpu.make_async_copy(stk, ext.at[pl.ds(RIM, rows), :, pl.ds(0, 256)], in_sem)
    own.start()
    start = pl.multiple_of(gy * rows, 8)
    kcopy = pltpu.make_async_copy(kxs.at[pl.ds(start, total), :], kxv, kx_sem)
    kcopy.start()

    barrier = pltpu.get_barrier_semaphore()
    for k in range(1, nx):
        pl.semaphore_signal(barrier, 1, device_id=(lax.rem(gx + k, nx), gy), device_id_type=MESH)
    for k in range(1, ny):
        pl.semaphore_signal(barrier, 1, device_id=(gx, lax.rem(gy + k, ny)), device_id_type=MESH)
    own.wait()
    lane = lanes((rows // 8, 40, 128))
    to_west = jnp.zeros((rows // 8, 40, 128), F32)
    to_east = jnp.zeros((rows // 8, 40, 128), F32)
    for j in range(8):
        here = (lane >= 16 * j) & (lane < 16 * j + 16)
        left = jnp.stack([ext[RIM + 8 * g + j, :, 0:128] for g in range(rows // 8)])
        right = jnp.stack([ext[RIM + 8 * g + j, :, 128:256] for g in range(rows // 8)])
        if j:
            left = pltpu.roll(left, 16 * j, 2)
        to_west = jnp.where(here, left, to_west)
        if j < 7:
            right = pltpu.roll(right, 16 * j + 16, 2)
        to_east = jnp.where(here, right, to_east)
    pack[0] = to_west
    pack[1] = to_east
    pl.semaphore_wait(barrier, nx + ny - 2)

    groups = rows // 8
    go_west = pltpu.make_async_remote_copy(
        pack.at[0], lon.at[0, pl.ds(1, groups)], lon_send.at[0], lon_recv.at[0],
        device_id=(west, gy), device_id_type=MESH)
    go_east = pltpu.make_async_remote_copy(
        pack.at[1], lon.at[1, pl.ds(1, groups)], lon_send.at[1], lon_recv.at[1],
        device_id=(east, gy), device_id_type=MESH)
    go_west.start()
    go_east.start()

    def strip(src, dst, size, chan, sem, peer):
        return pltpu.make_async_remote_copy(
            ext.at[pl.ds(src, size), chan, pl.ds(0, 256)],
            ext.at[pl.ds(dst, size), chan, pl.ds(0, 256)],
            lat_send.at[sem], lat_recv.at[sem], device_id=(gx, peer), device_id_type=MESH)

    vec, par = pl.ds(0, CH), pl.ds(CH, 24)
    to_s = [strip(RIM, top, RIM, vec, 0, south), strip(RIM, top, RIM - 2, par, 1, south)]
    to_n = [strip(rows, 0, RIM, vec, 2, north), strip(rows + 2, 2, RIM - 2, par, 3, north)]

    @pl.when(has_s)
    def _():
        for copy in to_s:
            copy.start()

    @pl.when(has_n)
    def _():
        for copy in to_n:
            copy.start()

    @pl.when(jnp.logical_not(has_s))
    def _():
        ext[0:RIM, :, 0:256] = jnp.zeros((RIM, 40, 256), F32)
        lon[:, 0] = jnp.zeros((2, 40, 128), F32)

    @pl.when(jnp.logical_not(has_n))
    def _():
        ext[top : top + RIM, :, 0:256] = jnp.zeros((RIM, 40, 256), F32)
        lon[:, groups + 1] = jnp.zeros((2, 40, 128), F32)

    go_west.wait_recv()
    go_east.wait_recv()
    cor_s = pltpu.make_async_remote_copy(
        lon.at[:, 1], lon.at[:, groups + 1], cor_send.at[0], cor_recv.at[0],
        device_id=(gx, south), device_id_type=MESH)
    cor_n = pltpu.make_async_remote_copy(
        lon.at[:, groups], lon.at[:, 0], cor_send.at[1], cor_recv.at[1],
        device_id=(gx, north), device_id_type=MESH)

    @pl.when(has_s)
    def _():
        cor_s.start()

    @pl.when(has_n)
    def _():
        cor_n.start()

    kcopy.wait()

    def unpack(g):
        from_e, from_w = lon[0, g], lon[1, g]
        lane2 = lanes((40, 128))
        for j in range(8):
            a = pltpu.roll(from_e, (128 - 16 * j) % 128, 1) if j else from_e
            b = pltpu.roll(from_w, 112 - 16 * j, 1) if j < 7 else from_w
            ext[g * 8 + j, :, 256:384] = jnp.where(
                lane2 < 16, a, jnp.where(lane2 >= 112, b, 0.0))

    @pl.loop(1, groups + 1)
    def _(g):
        unpack(g)

    @pl.when(has_s)
    def _():
        to_s[0].wait_send()
        to_s[1].wait_send()
        cor_s.wait_send()
        for copy in to_n:
            copy.wait_recv()
        cor_n.wait_recv()

    @pl.when(has_n)
    def _():
        to_n[0].wait_send()
        to_n[1].wait_send()
        cor_n.wait_send()
        for copy in to_s:
            copy.wait_recv()
        cor_s.wait_recv()

    unpack(0)
    unpack(groups + 1)

    two = 2.0 / HALF
    kind = lax.broadcasted_iota(jnp.int32, (8, 384), 0)
    by_kx = jnp.where(kind < 2, -two, 0.0)
    by_one = jnp.where((kind == 3) | (kind == 4), -0.5 * two, 0.0)
    eight = two * 8.0 / 12.0
    by_lon = jnp.where(kind == 0, eight, 0.0) + jnp.where(kind == 1, -eight, 0.0)
    by_lon = by_lon + jnp.where(kind == 2, -two / 12.0, 0.0)
    by_lat = jnp.where(kind == 3, eight, 0.0) + jnp.where(kind == 4, -eight, 0.0)
    by_lat = by_lat + jnp.where(kind == 5, -two / 12.0, 0.0)

    @pl.loop(2, total - 2)
    def _(r):
        kx = jnp.concatenate([kxv[pl.ds(r, 1), :]] * 3, axis=1)
        inside = jnp.where(kx > 0.0, 1.0, 0.0)
        wind = ext[r, 32:40, :]
        coef[r] = (kx * by_kx + inside * by_one + by_lon * wind[0:1, :] + by_lat * wind[1:2, :])
        diag = ext[r, CH : 2 * CH, :]
        ext[r, CH : 2 * CH, :] = (two * inside) * (diag + (2.0 - MID)) + (2.0 * two) * kx

    cm = coup[...] * (0.25 * two)
    cm = jnp.concatenate([jnp.concatenate([cm] * 4, axis=1)] * 4, axis=0)
    r4 = lax.broadcasted_iota(jnp.int32, (64, 64), 0) // 16
    c4 = lax.broadcasted_iota(jnp.int32, (64, 64), 1) // 16
    cm = jnp.where(r4 == c4, cm, 0.0)
    cm_hi = cm.astype(jnp.bfloat16)
    cm_lo = (cm - cm_hi.astype(F32)).astype(jnp.bfloat16)
    weights = jnp.concatenate([cm_hi, cm_hi, cm_lo], axis=1)

    def power(k):
        return ext.at[:, pl.ds(0, CH), :] if k == 0 else pwr.at[k - 1]

    lane4 = lanes((4, CH, 128))

    def advance(k):
        src, dst = power(k), power(k + 1)
        depth = k % BLOCK
        low = 2 * (depth + 1)
        count = (total - 2 * low) // 4
        prev = power(k - 1) if depth else None

        def body(g, carry):
            r0 = low + 4 * g
            mids = [src[pl.ds(r0, 4), :, 128 * t : 128 * t + 128] for t in range(3)]
            flat = jnp.concatenate([m.reshape(64, 128) for m in mids], axis=1)
            hi = flat.astype(jnp.bfloat16)
            lo = (flat - hi.astype(F32)).astype(jnp.bfloat16)
            mixed = jnp.dot(weights, jnp.concatenate([hi, lo, hi], axis=0),
                            preferred_element_type=F32)
            for t in range(3):
                cut = pl.ds(128 * t, 128)
                mid, nxt, prv = mids[t], mids[(t + 1) % 3], mids[(t + 2) % 3]
                e1 = pltpu.roll(jnp.where(lane4 < 1, nxt, mid), 127, 2)
                e2 = pltpu.roll(jnp.where(lane4 < 2, nxt, mid), 126, 2)
                w1 = pltpu.roll(jnp.where(lane4 >= 127, prv, mid), 1, 2)
                w2 = pltpu.roll(jnp.where(lane4 >= 126, prv, mid), 2, 2)
                n1 = src[pl.ds(r0 + 1, 4), :, cut]
                n2 = src[pl.ds(r0 + 2, 4), :, cut]
                s1 = src[pl.ds(r0 - 1, 4), :, cut]
                s2 = src[pl.ds(r0 - 2, 4), :, cut]
                cs = [coef[pl.ds(r0, 4), i : i + 1, cut] for i in range(6)]
                out = ext[pl.ds(r0, 4), CH : 2 * CH, cut] * mid
                out = out + mixed[:, 128 * t : 128 * t + 128].reshape(4, CH, 128)
                out = out + cs[0] * e1 + cs[1] * w1 + cs[2] * (e2 - w2)
                out = out + cs[3] * n1 + cs[4] * s1 + cs[5] * (n2 - s2)
                if prev is not None:
                    out = out - prev[pl.ds(r0, 4), :, cut]
                dst[pl.ds(r0, 4), :, cut] = out
            return carry

        lax.fori_loop(0, count, body, 0)

    for k in range(BLOCK):
        advance(k)

    half = power(BLOCK)

    def again(src, dst, sem, peer):
        return pltpu.make_async_remote_copy(
            half.at[pl.ds(src, RIM)], half.at[pl.ds(dst, RIM)],
            mid_send.at[sem], mid_recv.at[sem], device_id=(gx, peer), device_id_type=MESH)

    mid_s, mid_n = again(RIM, top, 0, south), again(rows, 0, 1, north)

    @pl.when(has_s)
    def _():
        mid_s.start()

    @pl.when(has_n)
    def _():
        mid_n.start()

    @pl.when(jnp.logical_not(has_s))
    def _():
        half[0:RIM] = jnp.zeros((RIM, CH, 384), F32)

    @pl.when(jnp.logical_not(has_n))
    def _():
        half[top : top + RIM] = jnp.zeros((RIM, CH, 384), F32)

    @pl.when(has_s)
    def _():
        mid_s.wait_send()
        mid_n.wait_recv()

    @pl.when(has_n)
    def _():
        mid_n.wait_send()
        mid_s.wait_recv()

    for k in range(BLOCK, ITERS):
        advance(k)

    pairs = [(i, k) for i in range(9) for k in range(i, 9)]

    def gram(r, sums):
        for o in range(2):
            for t in range(2):
                at = (r, pl.ds(8 * o, 8), pl.ds(128 * t, 128))
                vals = [power(k)[at] for k in range(9)]
                sums = [s + vals[i] * vals[k] for s, (i, k) in zip(sums, pairs)]
        return tuple(sums)

    sums = lax.fori_loop(RIM, top, gram, tuple(jnp.zeros((8, 128), F32) for _ in pairs))
    sums = dict(zip(pairs, sums))
    sub = lax.broadcasted_iota(jnp.int32, (16, 128), 0)
    lane16 = lanes((16, 128))
    folded = {p: jnp.sum(s, axis=0, keepdims=True) for p, s in sums.items()}
    mine = jnp.zeros((16, 128), F32)
    for k in range(9):
        col = jnp.zeros((16, 128), F32)
        for i in range(9):
            col = jnp.where(sub == i, folded[min(i, k), max(i, k)], col)
        mine = jnp.where(lane16 == k, jnp.sum(col, axis=1, keepdims=True), mine)

    def reduce_over(value, slots, send, recv, me, count, device):
        slots[me] = value
        copies = []
        for k in range(1, count):
            peer = lax.rem(me + k, count)
            copy = pltpu.make_async_remote_copy(
                slots.at[me], slots.at[me], send.at[k - 1], recv.at[me],
                device_id=device(peer), device_id_type=MESH)
            copy.start()
            copies.append(copy)
        for k in range(1, count):
            src = lax.rem(me + count - k, count)
            pltpu.make_async_remote_copy(
                slots.at[src], slots.at[src], send.at[k - 1], recv.at[src],
                device_id=device(src), device_id_type=MESH).wait_recv()
        value = slots[0]
        for k in range(1, count):
            value = value + slots[k]
        return value, copies

    value, sent = reduce_over(mine, gx_slots, gxs_send, gxs_recv, gx, nx, lambda p: (p, gy))
    value, more = reduce_over(value, gy_slots, gys_send, gys_recv, gy, ny, lambda p: (gx, p))

    plain = [jnp.broadcast_to(value[:, k : k + 1], (16, 128)) for k in range(9)]
    diag = jnp.zeros((16, 128), F32)
    for k in range(9):
        diag = jnp.where(sub == k, plain[k], diag)
    size = jnp.sqrt(diag)
    cols = [plain[k] + trial[k] * size * size[k : k + 1, :] for k in range(9)]
    q = gmres(cols)
    d = apply_a(q)
    q0 = jnp.broadcast_to(q[:, 0:1], (16, 128))
    d0 = jnp.broadcast_to(d[:, 0:1], (16, 128))
    left0 = jnp.where(sub == 0, 1.0, 0.0) - d0
    dq, dd = q - q0, d - d0
    bad_q = dot(dq, mat_vec(plain, dq, 8)) - TRUST**2 * dot(q0, mat_vec(plain, q0, 8))
    bad_d = dot(dd, mat_vec(plain, dd, 9)) - TRUST**2 * dot(left0, mat_vec(plain, left0, 9))
    fine = (bad_q <= 0.0) & (bad_d <= 0.0)
    flag[...] = jnp.broadcast_to(jnp.where(fine, 0.0, 1.0), (8, 128))

    qs = [q0[k : k + 1, :] for k in range(8)]
    ds = [left0[k : k + 1, :] for k in range(9)]

    @pl.loop(0, rows)
    def _(r):
        for t in range(2):
            cut = pl.ds(128 * t, 128)
            vals = [power(k)[r + RIM, :, cut] for k in range(9)]
            s = qs[0] * vals[0]
            e = ds[0] * vals[0]
            for k in range(1, 8):
                s = s + qs[k] * vals[k]
            for k in range(1, 9):
                e = e + ds[k] * vals[k]
            sol[r, :, cut] = s
            res[r, :, cut] = e

    go_west.wait_send()
    go_east.wait_send()
    for copy in sent + more:
        copy.wait_send()


def fused(nx, ny, stk, coup, lat_total):
    rows = stk.shape[0]
    total = rows + 2 * RIM
    vm = pl.BlockSpec(memory_space=pltpu.VMEM)
    hbm = pl.BlockSpec(memory_space=pl.ANY)
    dma = pltpu.SemaphoreType.DMA
    out = jax.ShapeDtypeStruct((rows, CH, 256), F32)
    return pl.pallas_call(
        functools.partial(kernel, nx, ny),
        out_shape=(out, out, jax.ShapeDtypeStruct((8, 128), F32)),
        in_specs=[hbm, vm, vm, hbm],
        out_specs=(vm, vm, vm),
        scratch_shapes=[
            pltpu.VMEM((total, 40, 384), F32),
            pltpu.VMEM((8, total, CH, 384), F32),
            pltpu.VMEM((total, 8, 384), F32),
            pltpu.VMEM((2, total // 8, 40, 128), F32),
            pltpu.VMEM((2, rows // 8, 40, 128), F32),
            pltpu.VMEM((total, 128), F32),
            pltpu.VMEM((nx, 16, 128), F32),
            pltpu.VMEM((ny, 16, 128), F32),
            dma, dma, dma((2,)), dma((2,)), dma((4,)), dma((4,)), dma((2,)), dma((2,)),
            dma((2,)), dma((2,)), dma((nx,)), dma((nx,)), dma((ny,)), dma((ny,)),
        ],
        compiler_params=pltpu.CompilerParams(
            collective_id=0, has_side_effects=True, vmem_limit_bytes=48 * 1024 * 1024),
        name="krylov",
    )(stk, coup, jnp.asarray(trial_table()), jnp.asarray(kx_table(lat_total)))


def shifted(cells, axis, dim, closed, width):
    count = lax.axis_size(axis)
    ends = count if closed else count - 1
    head = lax.slice_in_dim(cells, 0, width, axis=dim)
    tail = lax.slice_in_dim(cells, cells.shape[dim] - width, cells.shape[dim], axis=dim)
    return jnp.concatenate(
        [
            lax.ppermute(tail, axis, [(i, (i + 1) % count) for i in range(ends)]),
            cells,
            lax.ppermute(head, axis, [((i + 1) % count, i) for i in range(ends)]),
        ],
        axis=dim,
    )


def apply_plain(vec, damping, coupling, wind_lon, wind_lat, kx):
    wide = shifted(vec, "gx", 2, True, 2)
    tall = shifted(vec, "gy", 1, False, 2)
    e1, w1, e2, w2 = wide[:, :, 3:-1], wide[:, :, 1:-3], wide[:, :, 4:], wide[:, :, :-4]
    n1, s1, n2, s2 = tall[:, 3:-1], tall[:, 1:-3], tall[:, 4:], tall[:, :-4]
    mixed = jnp.einsum("ij,jab->iab", coupling, vec, precision=lax.Precision.HIGHEST)
    return (
        (1.0 + damping) * vec + 0.25 * mixed
        + kx * (2.0 * vec - e1 - w1) + 0.5 * (2.0 * vec - n1 - s1)
        + wind_lon * ((8.0 * (e1 - w1) - (e2 - w2)) / 12.0)
        + wind_lat * ((8.0 * (n1 - s1) - (n2 - s2)) / 12.0)
    )


def careful(forcing, damping, coupling, wind_lon, wind_lat):
    rows = forcing.shape[1]
    pos = (lax.axis_index("gy") * rows + jnp.arange(rows)).astype(F32)
    phi = -math.pi / 2 + (pos + 0.5) * (math.pi / (rows * lax.axis_size("gy")))
    kx = (0.5 / (jnp.cos(phi) ** 2 + 0.1))[:, None]
    operate = lambda v: apply_plain(v, damping, coupling, wind_lon, wind_lat, kx)
    every = ("gx", "gy")
    first = jnp.sqrt(lax.psum(jnp.sum(forcing * forcing), every) + 1.0)
    basis = jnp.zeros((ITERS,) + forcing.shape, F32).at[0].set(forcing / first)
    heights = jnp.zeros((ITERS + 1, ITERS), F32)

    def body(j, state):
        basis, heights = state
        w = operate(lax.dynamic_index_in_dim(basis, j, 0, keepdims=False))
        h = lax.psum(jnp.sum(basis * w[None], axis=(1, 2, 3)), every)
        w = w - jnp.sum(h[:, None, None, None] * basis, axis=0)
        below = jnp.sqrt(lax.psum(jnp.sum(w * w), every) + 1.0)
        col = jnp.concatenate([h, jnp.zeros((1,), F32)])
        col = jnp.where(jnp.arange(ITERS + 1) == j + 1, below, col)
        heights = lax.dynamic_update_slice(heights, col[:, None], (0, j))
        old = lax.dynamic_index_in_dim(basis, jnp.minimum(j + 1, ITERS - 1), 0, keepdims=False)
        new = jnp.where(j + 1 < ITERS, w / below, old)
        basis = lax.dynamic_update_index_in_dim(basis, new, jnp.minimum(j + 1, ITERS - 1), 0)
        return basis, heights

    basis, heights = lax.fori_loop(0, ITERS, body, (basis, heights))
    h = [[heights[i, j] for j in range(ITERS)] for i in range(ITERS + 1)]
    target = [first] + [jnp.zeros((), F32)] * ITERS
    turns = []
    for j in range(ITERS):
        for i in range(j):
            c, s = turns[i]
            h[i][j], h[i + 1][j] = c * h[i][j] + s * h[i + 1][j], c * h[i + 1][j] - s * h[i][j]
        radius = jnp.sqrt(h[j][j] * h[j][j] + h[j + 1][j] * h[j + 1][j])
        c, s = h[j][j] / radius, h[j + 1][j] / radius
        turns.append((c, s))
        h[j][j] = radius
        target[j], target[j + 1] = c * target[j] + s * target[j + 1], c * target[j + 1] - s * target[j]
    y = [None] * ITERS
    for j in reversed(range(ITERS)):
        part = target[j]
        for i in range(j + 1, ITERS):
            part = part - h[j][i] * y[i]
        y[j] = part / h[j][j]
    weights = jnp.stack(y)
    answer = jnp.sum(weights[:, None, None, None] * basis, axis=0)
    return answer, forcing - operate(answer)


def per_device(nx, ny, forcing, damping, coupling, wind_lon, wind_lat):
    channels, rows, cols = forcing.shape
    pad = jnp.zeros((6, rows, cols), F32)
    stk = jnp.concatenate([forcing, damping, wind_lon[None], wind_lat[None], pad], axis=0)
    stk = jnp.transpose(stk, (1, 0, 2))
    sol, res, flag = fused(nx, ny, stk, coupling, rows * ny)
    trusted = jnp.max(flag) == 0.0
    back = lambda: (jnp.transpose(sol, (1, 0, 2)), jnp.transpose(res, (1, 0, 2)))
    slow = lambda: careful(forcing, damping, coupling, wind_lon, wind_lat)
    return lax.cond(trusted, back, slow)


def solution(mesh):
    nx, ny = mesh.shape["gx"], mesh.shape["gy"]
    in_specs = (P(None, "gy", "gx"), P(None, "gy", "gx"), P(), P("gy", "gx"), P("gy", "gx"))
    out_specs = (P(None, "gy", "gx"), P(None, "gy", "gx"))
    return jax.shard_map(
        functools.partial(per_device, nx, ny),
        mesh=mesh, in_specs=in_specs, out_specs=out_specs, check_vma=False,
    )
```

time: 704 us -> 69.4 us (0.10); the launches traced: 691 us -> 68.6 us
  blocking collectives: 288 us -> 0 us
  other arithmetic: 128 us -> 0.6 us
  between operations: 117 us -> 1.41 us
  local copies, waits for them, and re-layouts: 94.7 us -> 13 us
  Pallas kernels: 0 us -> 53.3 us
  matrix products: 41.7 us -> 0 us
  waiting for transfers between devices: 13.4 us -> 0 us
  starting transfers between devices: 8.48 us -> 0 us
    psum x36 -> x0, blocking collectives: 288 us -> none  [one_axis_at_a_time(): value = lax.psum(value, axis)]
    pallas_call x0 -> x1, Pallas kernels: none -> 53.3 us  [fused(): pl.pallas_call(functools.partial(kernel, nx, ny), out_shape=(out, out, ja...]
    another operation x41 -> x0, other arithmetic: 44.4 us -> none
    dot_general x9 -> x0, matrix products: 41.7 us -> none  [apply_core(): jnp.einsum('ij,jab->iab', coupling, centre, precision=lax.Precision.HIGHEST)]
    div x15 -> x0, other arithmetic: 39.9 us -> none  [the longest x7 39.6 us: per_device(): krylov.append((applied / subdiag, rim_new))]
    slice x64 -> x0, local copies, waits for them, and re-layouts: 33.7 us -> none  [the longest x25 15.2 us: least_squares(): lower_val = column_vec[earlier + 1]]
    scatter x123 -> x0, local copies, waits for them, and re-layouts: 27.3 us -> none  [the longest x16 11.9 us: per_device(): heights.at[:column + 1, column].set(coeffs).at[column + 1, column]]
    reduce_sum x22 -> x0, other arithmetic: 23.5 us -> none  [the longest x7 17.7 us: per_device(): jnp.sum(crop_rim(vector, rim_vec, 0) * applied_in)]
  transfers between devices with their start and end apart: 4 -> 0, of which waited for: 2 -> 0; matrix products, arithmetic and copies ran while one was open for 2% -> 0% of each run, Pallas kernels for 0% -> 0%
where the time goes in v1:
time: 69.4 us; the launch traced here: 68.6 us
  Pallas kernels  53.3 us (77%)
  local copies, waits for them, and re-layouts  13 us (19%)
  between operations  1.41 us (2%)
    pallas_call x1, Pallas kernels, fused(): pl.pallas_call(functools.partial(kernel, nx, ny), out_shape=(out, out, ja...  53.3 us
    unnamed x17, local copies, waits for them, and re-layouts  4.44 us
    cond x2, local copies, waits for them, and re-layouts, per_device(): return lax.cond(trusted, back, slow)  3.68 us
    concatenate x1, local copies, waits for them, and re-layouts, per_device(): jnp.concatenate([forcing, damping, wind_lon[None], wind_lat[None], pad],...  2.09 us
    broadcast_in_dim x1, local copies, waits for them, and re-layouts, per_device(): wind_lon[None]  1.39 us
    broadcast_in_dim x1, local copies, waits for them, and re-layouts, per_device(): wind_lat[None]  1.39 us

profile of v1, /device:TPU:0, one launch (start us, length us, event | category | flops | bytes accessed | tf_op | source)
XLA Modules:
  0.0 68.6 jit_solution(14776466659432855590)
XLA Ops:
  0.6 0.0 copy-start.1
  0.6 0.0 copy-start
  0.7 0.0 copy-start.3
  0.7 0.0 copy-start.4
  0.7 0.0 copy-start.5
  0.7 0.0 copy-start.6
  0.7 1.4 %copy.11 = f32[16,32,256]{2,0,1:T(8,128)S(1)} copy(f32[16,32,256]{2,1,0:T(8,128)} %param.13) | data formatting | bytes 1048576 | tf_op args[0]
  2.2 2.1 %copy.12 = f32[16,32,256]{2,0,1:T(8,128)} copy(f32[16,32,256]{2,1,0:T(8,128)} %param.14) | data formatting | bytes 1048576 | tf_op args[1]
  4.3 1.4 %broadcast_in_dim.45 = f32[1,32,256]{2,0,1:T(1,128)} reshape(f32[32,256]{1,0:T(8,128)} %param.16) | data formatting | bytes 65536 | tf_op jit(solution)/shard_map/broadcast_in_dim | solution.py:552
  5.7 1.4 %broadcast_in_dim.46 = f32[1,32,256]{2,0,1:T(1,128)} reshape(f32[32,256]{1,0:T(8,128)} %param.17) | data formatting | bytes 65536 | tf_op jit(solution)/shard_map/broadcast_in_dim | solution.py:552
  7.1 2.1 %concatenate.77 = f32[40,32,256]{2,0,1:T(8,128)S(1)} concatenate(f32[16,32,256]{2,0,1:T(8,128)S(1)} %copy.11, f32[16,32,256]{2,0,1:T(8,128)} %copy.12, f32[1,32,256]{2,0,1:T(1,128)} %broadcast_in_dim.45, f32[1,32,256]{2,0,1:T(1,128)} %broadcast_in_dim.46, f32[6,32,256]{2,0,1:T(8,128)S(1)} %broadcast_in_dim.47), dimensions={0} | concatenate | bytes 2621440 | tf_op jit(solution)/shard_map/concatenate | solution.py:552
  9.2 0.0 copy-done.1
  9.2 0.0 copy-done
  9.2 53.3 %krylov.1 = (f32[32,16,256]{2,1,0:T(8,128)S(1)}, f32[32,16,256]{2,1,0:T(8,128)}, f32[8,128]{1,0:T(8,128)S(1)}) custom-call(f32[32,40,256]{2,1,0:T(8,128)S(1)} %bitcast.100, f32[16,16]{1,0:T(8,128)} %coup.1, f32[9,16,128]{2,1,0:T(8,128)S(1)} %copy-done.1, f32[528,128]{1,0:T(8,128)S(1)} %copy-done), custom_call_target="tpu_custom_call" | custom-call | tf_op jit(solution)/shard_map/krylov/pallas_call | solution.py:448
  62.5 0.8 %copy.39 = f32[32,16,256]{2,1,0:T(8,128)} copy(f32[32,16,256]{2,1,0:T(8,128)S(1)} %get-tuple-element.402) | data formatting | bytes 1048576
  63.3 0.6 reduce_max.9
  64.6 0.0 copy-done.3
  64.6 0.0 copy-done.4
  64.6 0.0 copy-done.5
  64.6 0.0 copy-done.6
  64.6 1.6 %conditional.1 = (f32[16,32,256]{2,0,1:T(8,128)}, f32[16,32,256]{2,1,0:T(8,128)S(1)}) conditional(s32[]{:T(128)} %convert_element_type.10, (f32[16,32,256]{2,1,0:T(8,128)S(1)}, f32[16,32,256]{2,1,0:T(8,128)S(1)}, f32[16,16]{1,0:T(8,128)}, f32[32,256]{1,0:T(8,128)S(1)}, f32[32,256]{1,0:T(8,128)S(1)}) %tuple.121, (f32[32,16,256]{2,1,0:T(8,128)}, ...), branch_computations={%region_1.12_spmd, %region_12.13_spmd} | conditional | flops 66224676 | bytes 50728124 | solution.py:558
  64.9 1.4 %copy.18 = f32[16,32,256]{2,1,0:T(8,128)S(1)} copy(f32[16,32,256]{2,0,1:T(8,128)} %bitcast.101) | data formatting | bytes 1048576 | tf_op jit(solution)/shard_map/cond | solution.py:558
  66.2 0.0 copy-start.7
  66.2 2.3 %copy.15 = f32[16,32,256]{2,1,0:T(8,128)} copy(f32[16,32,256]{2,0,1:T(8,128)} %get-tuple-element.206) | data formatting | bytes 1048576 | tf_op jit(solution)/shard_map/cond | solution.py:558
  68.6 0.0 copy-done.7
  (1 shorter events, 0.0 us)
Async XLA Ops:
  0.6 8.6 %copy-start.1 = (f32[9,16,128]{2,1,0:T(8,128)S(1)}, f32[9,16,128]{2,1,0:T(8,128)}, u32[]{:S(2)}) copy-start(f32[9,16,128]{2,1,0:T(8,128)} %constant.163.clone.trial) | copy-start | bytes 221188
  0.6 8.6 %copy-start = (f32[528,128]{1,0:T(8,128)S(1)}, f32[528,128]{1,0:T(8,128)}, u32[]{:S(2)}) copy-start(f32[528,128]{1,0:T(8,128)} %constant.164.clone.kxs) | copy-start | bytes 811012
  0.7 63.9 %copy-start.3 = (f32[16,32,256]{2,1,0:T(8,128)S(1)}, f32[16,32,256]{2,1,0:T(8,128)}, u32[]{:S(2)}) copy-start(f32[16,32,256]{2,1,0:T(8,128)} %param.13) | copy-start | bytes 1572868
  0.7 63.9 %copy-start.4 = (f32[16,32,256]{2,1,0:T(8,128)S(1)}, f32[16,32,256]{2,1,0:T(8,128)}, u32[]{:S(2)}) copy-start(f32[16,32,256]{2,1,0:T(8,128)} %param.14) | copy-start | bytes 1572868
  0.7 63.9 %copy-start.5 = (f32[32,256]{1,0:T(8,128)S(1)}, f32[32,256]{1,0:T(8,128)}, u32[]{:S(2)}) copy-start(f32[32,256]{1,0:T(8,128)} %param.16) | copy-start | bytes 98308
  0.7 63.9 %copy-start.6 = (f32[32,256]{1,0:T(8,128)S(1)}, f32[32,256]{1,0:T(8,128)}, u32[]{:S(2)}) copy-start(f32[32,256]{1,0:T(8,128)} %param.17) | copy-start | bytes 98308
  66.2 2.3 %copy-start.7 = (f32[16,32,256]{2,1,0:T(8,128)}, f32[16,32,256]{2,1,0:T(8,128)S(1)}, u32[]{:S(2)}) copy-start(f32[16,32,256]{2,1,0:T(8,128)S(1)} %get-tuple-element.208) | copy-start | bytes 1572868

commit v2 on v1

v2 whole, which is shorter than its diff:
```python
import functools
import math

import jax
import jax.numpy as jnp
import numpy as np
from jax import lax
from jax.experimental import pallas as pl
from jax.experimental.pallas import tpu as pltpu
from jax.experimental.layout import Layout, with_layout_constraint
from jax.sharding import PartitionSpec as P

ITERS = 8
CH = 16
RIM = 8
LOW, HIGH = 1.0, 16.0
MID, HALF = (LOW + HIGH) / 2, (HIGH - LOW) / 2
BLOCK = 4
NOISE = 1.2e-7
TRUST = 1.0e-4
MESH = pl.DeviceIdType.MESH
F32 = jnp.float32


def trial_table():
    rng = np.random.default_rng(7)
    draw = rng.choice([-1.0, 1.0], size=(9, 16, 128)) * NOISE
    table = np.zeros((9, 16, 128), np.float32)
    for i in range(9):
        for k in range(i, 9):
            table[i, k] = draw[i, k]
            table[k, i] = draw[i, k]
    table[:, :, 0] = 0.0
    return table


def kx_table(lat_total):
    row = np.arange(lat_total) + 0.5
    phi = -math.pi / 2 + row * (math.pi / lat_total)
    table = np.zeros((lat_total + 2 * RIM, 128), np.float32)
    table[RIM : RIM + lat_total] = (0.5 / (np.cos(phi) ** 2 + 0.1))[:, None]
    return table


def lanes(shape):
    return lax.broadcasted_iota(jnp.int32, shape, len(shape) - 1)


def apply_a(vec):
    sub = lax.broadcasted_iota(jnp.int32, vec.shape, 0)
    up = pltpu.roll(vec, 1, 0)
    kept = jnp.where((sub == 0) | (sub == BLOCK), 0.0, vec)
    down = pltpu.roll(kept, 15, 0)
    return MID * vec + (HALF / 2) * (up + down)


def mat_vec(cols, vec, count):
    total = cols[0] * vec[0:1, :]
    for k in range(1, count):
        total = total + cols[k] * vec[k : k + 1, :]
    return total


def dot(a, b):
    return jnp.sum(a * b, axis=0, keepdims=True)


def gmres(cols):
    sub = lax.broadcasted_iota(jnp.int32, (16, 128), 0)
    first = jnp.sqrt(cols[0][0:1, :] + 1.0)
    basis = [jnp.where(sub == 0, 1.0, 0.0) / first]
    target = first
    targets = []
    columns = []
    turns = []
    for j in range(ITERS):
        w = apply_a(basis[j])
        u = mat_vec(cols, w, j + 2)
        h = [dot(v, u) for v in basis]
        for i in range(j + 1):
            w = w - h[i] * basis[i]
        norm = dot(w, mat_vec(cols, w, j + 2))
        below = jnp.sqrt(jnp.maximum(norm, 0.0) + 1.0)
        if j + 1 < ITERS:
            basis.append(w / below)
        col = list(h)
        for i, (c, s) in enumerate(turns):
            if i + 1 <= j:
                col[i], col[i + 1] = c * col[i] + s * col[i + 1], c * col[i + 1] - s * col[i]
        radius = jnp.sqrt(col[j] * col[j] + below * below)
        inv = 1.0 / radius
        c, s = col[j] * inv, below * inv
        turns.append((c, s))
        col[j] = radius
        columns.append((col, inv))
        targets.append(c * target)
        target = -s * target
    y = [None] * ITERS
    for j in reversed(range(ITERS)):
        y[j] = targets[j] * columns[j][1]
        for i in range(j):
            targets[i] = targets[i] - columns[j][0][i] * y[j]
    q = basis[0] * y[0]
    for j in range(1, ITERS):
        q = q + basis[j] * y[j]
    return q


def kernel(
    nx, ny, forc, damp, wlon, wlat, coup, trial, kxs, sol, res, flag,
    *scratch,
):
    pwr, scratch = scratch[:ITERS], scratch[ITERS:]
    (ext, coef, main, wind, lon, pack, kxv, mix, made, rims, gx_slots, gy_slots, outs,
     in_sem, kx_sem, lon_send, lon_recv, lat_send, lat_recv, cor_send, cor_recv,
     mid_send, mid_recv, gxs_send, gxs_recv, gys_send, gys_recv, out_sem) = scratch
    gx, gy = lax.axis_index("gx"), lax.axis_index("gy")
    rows = forc.shape[1]
    top = RIM + rows
    total = rows + 2 * RIM
    groups = rows // 8
    east, west = lax.rem(gx + 1, nx), lax.rem(gx + nx - 1, nx)
    north, south = gy + 1, gy - 1
    has_n, has_s = gy < ny - 1, gy > 0
    no_n, no_s = jnp.logical_not(has_n), jnp.logical_not(has_s)

    loads = []
    for c in range(CH):
        for n, src in enumerate((forc, damp)):
            loads.append(pltpu.make_async_copy(
                src.at[c], ext.at[pl.ds(RIM, rows), CH * n + c, pl.ds(0, 256)],
                in_sem.at[CH * n + c]))
    for n, src in enumerate((wlon, wlat)):
        loads.append(pltpu.make_async_copy(
            src, wind.at[n, pl.ds(RIM, rows), pl.ds(0, 256)], in_sem.at[2 * CH + n]))
    start = pl.multiple_of(gy * rows, 8)
    loads.append(pltpu.make_async_copy(kxs.at[pl.ds(start, total), :], kxv, kx_sem))
    for copy in loads:
        copy.start()

    barrier = pltpu.get_barrier_semaphore()
    for k in range(1, nx):
        pl.semaphore_signal(barrier, 1, device_id=(lax.rem(gx + k, nx), gy), device_id_type=MESH)
    for k in range(1, ny):
        pl.semaphore_signal(barrier, 1, device_id=(gx, lax.rem(gy + k, ny)), device_id_type=MESH)
    for copy in loads:
        copy.wait()

    def turn(value, by):
        by = by % 128
        return pltpu.roll(value, by, value.ndim - 1) if by else value

    lane32, lane8 = lanes((2 * CH, 128)), lanes((8, 128))

    @pl.loop(0, groups)
    def _(g):
        for side in range(2):
            shift, cut = (0, pl.ds(0, 128)) if side == 0 else (16, pl.ds(128, 128))
            out = jnp.zeros((2 * CH, 128), F32)
            for j in range(8):
                here = (lane32 >= 16 * j) & (lane32 < 16 * j + 16)
                out = jnp.where(here, turn(ext[RIM + 8 * g + j, :, cut], 16 * j + shift), out)
            pack[side, g, 0 : 2 * CH, :] = out
            at = pl.ds(pl.multiple_of(RIM + 8 * g, 8), 8)
            a = turn(wind[0, at, cut], shift)
            b = turn(wind[1, at, cut], 16 + shift)
            pack[side, g, 2 * CH :, :] = jnp.where(lane8 < 16, a, b)

    pl.semaphore_wait(barrier, nx + ny - 2)

    go_west = pltpu.make_async_remote_copy(
        pack.at[0], lon.at[0, pl.ds(1, groups)], lon_send.at[0], lon_recv.at[0],
        device_id=(west, gy), device_id_type=MESH)
    go_east = pltpu.make_async_remote_copy(
        pack.at[1], lon.at[1, pl.ds(1, groups)], lon_send.at[1], lon_recv.at[1],
        device_id=(east, gy), device_id_type=MESH)
    go_west.start()
    go_east.start()

    def strip(ref, src, dst, size, chan, sem, peer):
        return pltpu.make_async_remote_copy(
            ref.at[pl.ds(src, size), chan, pl.ds(0, 256)],
            ref.at[pl.ds(dst, size), chan, pl.ds(0, 256)],
            lat_send.at[sem], lat_recv.at[sem], device_id=(gx, peer), device_id_type=MESH)

    def breeze(src, dst, sem, peer):
        return pltpu.make_async_remote_copy(
            wind.at[:, pl.ds(src, 8), pl.ds(0, 256)], wind.at[:, pl.ds(dst, 8), pl.ds(0, 256)],
            lat_send.at[sem], lat_recv.at[sem], device_id=(gx, peer), device_id_type=MESH)

    vec, par = pl.ds(0, CH), pl.ds(CH, CH)
    to_s = [breeze(RIM, top, 4, south), strip(ext, RIM, top, RIM, vec, 0, south),
            strip(ext, RIM, top, RIM - 2, par, 1, south)]
    to_n = [breeze(rows, 0, 5, north), strip(ext, rows, 0, RIM, vec, 2, north),
            strip(ext, rows + 2, 2, RIM - 2, par, 3, north)]

    @pl.when(has_s)
    def _():
        for copy in to_s:
            copy.start()

    @pl.when(has_n)
    def _():
        for copy in to_n:
            copy.start()

    for missing, row, slot in ((no_s, 0, 0), (no_n, top, groups + 1)):
        @pl.when(missing)
        def _():
            ext[row : row + RIM, 0 : 2 * CH, 0:256] = jnp.zeros((RIM, 2 * CH, 256), F32)
            wind[:, row : row + RIM, 0:256] = jnp.zeros((2, RIM, 256), F32)
            lon[:, slot] = jnp.zeros((2, 40, 128), F32)

    go_west.wait_recv()
    go_east.wait_recv()
    cor_s = pltpu.make_async_remote_copy(
        lon.at[:, 1], lon.at[:, groups + 1], cor_send.at[0], cor_recv.at[0],
        device_id=(gx, south), device_id_type=MESH)
    cor_n = pltpu.make_async_remote_copy(
        lon.at[:, groups], lon.at[:, 0], cor_send.at[1], cor_recv.at[1],
        device_id=(gx, north), device_id_type=MESH)

    @pl.when(has_s)
    def _():
        cor_s.start()

    @pl.when(has_n)
    def _():
        cor_n.start()

    two = 2.0 / HALF
    kind = lax.broadcasted_iota(jnp.int32, (8, 128), 0)
    by_kx = jnp.where(kind < 2, -two, 0.0)
    by_one = jnp.where((kind == 3) | (kind == 4), -0.5 * two, 0.0)
    eight = two * 8.0 / 12.0
    by_lon = jnp.where(kind == 0, eight, 0.0) + jnp.where(kind == 1, -eight, 0.0)
    by_lon = by_lon + jnp.where(kind == 2, -two / 12.0, 0.0)
    by_lat = jnp.where(kind == 3, eight, 0.0) + jnp.where(kind == 4, -eight, 0.0)
    by_lat = by_lat + jnp.where(kind == 5, -two / 12.0, 0.0)

    def merge(from_e, from_w):
        at = lanes(from_e.shape)
        return jnp.where(at < 16, from_e, jnp.where(at >= 112, from_w, 0.0))

    def prepare(g):
        at = pl.ds(pl.multiple_of(8 * g, 8), 8)
        for j in range(8):
            ext[8 * g + j, 0 : 2 * CH, 256:384] = merge(
                turn(lon[0, g, 0 : 2 * CH, :], -16 * j), turn(lon[1, g, 0 : 2 * CH, :], 112 - 16 * j))
        for n in range(2):
            wind[n, at, 256:384] = merge(
                turn(lon[0, g, 2 * CH :, :], -16 * n), turn(lon[1, g, 2 * CH :, :], 112 - 16 * n))
        kx8 = kxv[at, :]
        in8 = jnp.where(kx8 > 0.0, 1.0, 0.0)
        for t in range(3):
            cut = pl.ds(128 * t, 128)
            lon8, lat8 = wind[0, at, cut], wind[1, at, cut]
            for j in range(8):
                one = slice(j, j + 1)
                coef[8 * g + j, :, cut] = (
                    kx8[one] * by_kx + in8[one] * by_one + by_lon * lon8[one] + by_lat * lat8[one])
                diag = ext[8 * g + j, CH : 2 * CH, cut]
                gain, base = two * in8[one], (two * (2.0 - MID)) * in8[one] + (2.0 * two) * kx8[one]
                main[8 * g + j, :, cut] = diag * gain + base

    @pl.loop(1, groups + 1)
    def _(g):
        prepare(g)

    cm = coup[...] * (0.25 * two)
    cm = jnp.concatenate([jnp.concatenate([cm] * 4, axis=1)] * 4, axis=0)
    r4 = lax.broadcasted_iota(jnp.int32, (64, 64), 0) // 16
    c4 = lax.broadcasted_iota(jnp.int32, (64, 64), 1) // 16
    cm = jnp.where(r4 == c4, cm, 0.0)
    cm_hi = cm.astype(jnp.bfloat16)
    cm_lo = (cm - cm_hi.astype(F32)).astype(jnp.bfloat16)
    weights = jnp.concatenate([cm_hi, cm_hi, cm_lo], axis=1)

    def power(k):
        return ext.at[:, pl.ds(0, CH), :] if k == 0 else pwr[k - 1]

    lane4 = lanes((4, CH, 128))

    def couple(src, r0):
        mids = [src[pl.ds(r0, 4), :, 128 * t : 128 * t + 128] for t in range(3)]
        flat = jnp.concatenate([m.reshape(64, 128) for m in mids], axis=1)
        hi = flat.astype(jnp.bfloat16)
        lo = (flat - hi.astype(F32)).astype(jnp.bfloat16)
        return jnp.dot(weights, jnp.concatenate([hi, lo, hi], axis=0), preferred_element_type=F32)

    def stencil(k, r0, mixed):
        src, dst = power(k), power(k + 1)
        prev = power(k - 1) if k % BLOCK else None
        mids = [src[pl.ds(r0, 4), :, 128 * t : 128 * t + 128] for t in range(3)]
        for t in range(3):
            cut = pl.ds(128 * t, 128)
            mid, nxt, prv = mids[t], mids[(t + 1) % 3], mids[(t + 2) % 3]
            e1 = pltpu.roll(jnp.where(lane4 < 1, nxt, mid), 127, 2)
            e2 = pltpu.roll(jnp.where(lane4 < 2, nxt, mid), 126, 2)
            w1 = pltpu.roll(jnp.where(lane4 >= 127, prv, mid), 1, 2)
            w2 = pltpu.roll(jnp.where(lane4 >= 126, prv, mid), 2, 2)
            n1 = src[pl.ds(r0 + 1, 4), :, cut]
            n2 = src[pl.ds(r0 + 2, 4), :, cut]
            s1 = src[pl.ds(r0 - 1, 4), :, cut]
            s2 = src[pl.ds(r0 - 2, 4), :, cut]
            cs = [coef[pl.ds(r0, 4), i : i + 1, cut] for i in range(6)]
            out = main[pl.ds(r0, 4), :, cut] * mid
            out = out + mixed[:, 128 * t : 128 * t + 128].reshape(4, CH, 128)
            out = out + cs[0] * e1 + cs[1] * w1 + cs[2] * (e2 - w2)
            out = out + cs[3] * n1 + cs[4] * s1 + cs[5] * (n2 - s2)
            if prev is not None:
                out = out - prev[pl.ds(r0, 4), :, cut]
            dst[pl.ds(r0, 4), :, cut] = out

    def inner(k):
        m = k % BLOCK + 1
        low, count = RIM + 2 * m, (rows - 4 * m) // 4
        mix[0] = couple(power(k), low)

        def body(g, carry):
            r0 = low + 4 * g
            ahead = couple(power(k), jnp.minimum(r0 + 4, low + 4 * (count - 1)))
            stencil(k, r0, mix[g % 2])
            mix[(g + 1) % 2] = ahead
            return carry

        lax.fori_loop(0, count, body, 0)

    def outer(k):
        m = k % BLOCK + 1
        for r0 in (2 * m, 2 * m + 4, top - 2 * m, top - 2 * m + 4):
            stencil(k, r0, couple(power(k), r0))

    for k in range(BLOCK):
        inner(k)

    @pl.when(has_s)
    def _():
        for copy in to_s:
            copy.wait_send()
        cor_s.wait_send()
        for copy in to_n:
            copy.wait_recv()
        cor_n.wait_recv()

    @pl.when(has_n)
    def _():
        for copy in to_n:
            copy.wait_send()
        cor_n.wait_send()
        for copy in to_s:
            copy.wait_recv()
        cor_s.wait_recv()

    prepare(0)
    prepare(groups + 1)
    for k in range(BLOCK):
        outer(k)

    half = power(BLOCK)
    lane16 = lanes((CH, 128))
    for side, row in ((0, RIM), (1, rows)):
        out = jnp.zeros((CH, 128), F32)
        for j in range(8):
            here = (lane16 >= 16 * j) & (lane16 < 16 * j + 16)
            out = jnp.where(here, turn(half[row + j, :, 256:384], 16 * j + 8), out)
        made[side] = out

    def again(src, dst, sem, peer):
        return pltpu.make_async_remote_copy(
            half.at[pl.ds(src, RIM), :, pl.ds(0, 256)], half.at[pl.ds(dst, RIM), :, pl.ds(0, 256)],
            mid_send.at[sem], mid_recv.at[sem], device_id=(gx, peer), device_id_type=MESH)

    def also(src, dst, sem, peer):
        return pltpu.make_async_remote_copy(
            made.at[src], rims.at[dst], mid_send.at[sem], mid_recv.at[sem],
            device_id=(gx, peer), device_id_type=MESH)

    mid_s = [also(0, 1, 2, south), again(RIM, top, 0, south)]
    mid_n = [also(1, 0, 3, north), again(rows, 0, 1, north)]

    @pl.when(has_s)
    def _():
        for copy in mid_s:
            copy.start()

    @pl.when(has_n)
    def _():
        for copy in mid_n:
            copy.start()

    for missing, row, slot in ((no_s, 0, 0), (no_n, top, 1)):
        @pl.when(missing)
        def _():
            half[row : row + RIM, :, 0:256] = jnp.zeros((RIM, CH, 256), F32)
            rims[slot] = jnp.zeros((CH, 128), F32)

    for k in range(BLOCK, ITERS):
        inner(k)

    pairs = [(i, k) for i in range(9) for k in range(i, 9)]

    def gram(r, sums):
        for o in range(2):
            for t in range(2):
                at = (r, pl.ds(8 * o, 8), pl.ds(128 * t, 128))
                vals = [power(k)[at] for k in range(9)]
                sums = [s + vals[i] * vals[k] for s, (i, k) in zip(sums, pairs)]
        return tuple(sums)

    sums = tuple(jnp.zeros((8, 128), F32) for _ in pairs)
    sums = lax.fori_loop(2 * RIM, top - RIM, gram, sums)

    @pl.when(has_s)
    def _():
        for copy in mid_s:
            copy.wait_send()
        for copy in mid_n:
            copy.wait_recv()

    @pl.when(has_n)
    def _():
        for copy in mid_n:
            copy.wait_send()
        for copy in mid_s:
            copy.wait_recv()

    for side, row in ((0, 0), (1, top)):
        for j in range(8):
            half[row + j, :, 256:384] = turn(rims[side], -16 * j - 8)
    for k in range(BLOCK, ITERS):
        outer(k)
    sums = lax.fori_loop(RIM, 2 * RIM, gram, sums)
    sums = lax.fori_loop(top - RIM, top, gram, sums)

    sums = dict(zip(pairs, sums))
    folded = {p: jnp.sum(s, axis=0, keepdims=True) for p, s in sums.items()}
    sub8 = lax.broadcasted_iota(jnp.int32, (8, 128), 0)
    mine = jnp.zeros((8, 128), F32)
    for k in range(10):
        col = jnp.zeros((8, 128), F32)
        if k < 9:
            for i in range(8):
                col = jnp.where(sub8 == i, folded[min(i, k), max(i, k)], col)
        else:
            col = jnp.where(sub8 == 0, folded[8, 8], col)
        mine = jnp.where(lane8 == k, jnp.sum(col, axis=1, keepdims=True), mine)

    def reduce_over(value, slots, send, recv, me, count, device):
        slots[me] = value
        copies = []
        for k in range(1, count):
            peer = lax.rem(me + k, count)
            copy = pltpu.make_async_remote_copy(
                slots.at[me], slots.at[me], send.at[k - 1], recv.at[me],
                device_id=device(peer), device_id_type=MESH)
            copy.start()
            copies.append(copy)
        for k in range(1, count):
            src = lax.rem(me + count - k, count)
            pltpu.make_async_remote_copy(
                slots.at[src], slots.at[src], send.at[k - 1], recv.at[src],
                device_id=device(src), device_id_type=MESH).wait_recv()
        parts = [slots[k] for k in range(count)]
        while len(parts) > 1:
            parts = [sum(parts[i : i + 2][1:], parts[i]) for i in range(0, len(parts), 2)]
        return parts[0], copies

    value, sent = reduce_over(mine, gx_slots, gxs_send, gxs_recv, gx, nx, lambda p: (p, gy))
    value, more = reduce_over(value, gy_slots, gys_send, gys_recv, gy, ny, lambda p: (gx, p))

    upper = [jnp.broadcast_to(value[:, k : k + 1], (8, 128)) for k in range(10)]
    lower = [upper[8][k : k + 1, :] for k in range(8)] + [upper[9][0:1, :]]
    plain = [jnp.concatenate([u, jnp.where(sub8 == 0, w, 0.0)]) for u, w in zip(upper, lower)]
    sub = lax.broadcasted_iota(jnp.int32, (16, 128), 0)
    diag = jnp.zeros((16, 128), F32)
    for k in range(9):
        diag = jnp.where(sub == k, plain[k], diag)
    size = jnp.sqrt(diag)
    cols = [plain[k] + trial[k] * size * size[k : k + 1, :] for k in range(9)]
    q = gmres(cols)
    d = apply_a(q)
    q0 = jnp.broadcast_to(q[:, 0:1], (16, 128))
    d0 = jnp.broadcast_to(d[:, 0:1], (16, 128))
    left0 = jnp.where(sub == 0, 1.0, 0.0) - d0
    dq, dd = q - q0, d - d0
    bad_q = dot(dq, mat_vec(plain, dq, 8)) - TRUST**2 * dot(q0, mat_vec(plain, q0, 8))
    bad_d = dot(dd, mat_vec(plain, dd, 9)) - TRUST**2 * dot(left0, mat_vec(plain, left0, 9))
    fine = (bad_q <= 0.0) & (bad_d <= 0.0)
    flag[0, 0] = jnp.max(jnp.where(fine, 0.0, 1.0))

    qs = [q0[k : k + 1, :] for k in range(8)]
    ds = [left0[k : k + 1, :] for k in range(9)]
    stores = []
    part = rows // 2
    for h in range(2):
        @pl.loop(h * part, (h + 1) * part)
        def _(r):
            for t in range(2):
                cut = pl.ds(128 * t, 128)
                vals = [power(k)[r + RIM, :, cut] for k in range(9)]
                s = qs[0] * vals[0]
                e = ds[0] * vals[0]
                for k in range(1, 8):
                    s = s + qs[k] * vals[k]
                for k in range(1, 9):
                    e = e + ds[k] * vals[k]
                outs[0, r, :, cut] = s
                outs[1, r, :, cut] = e

        for c in range(CH):
            for n, dst in enumerate((sol, res)):
                copy = pltpu.make_async_copy(
                    outs.at[n, pl.ds(h * part, part), c, :],
                    dst.at[c, pl.ds(h * part, part), :], out_sem.at[h, n, c])
                copy.start()
                stores.append(copy)

    go_west.wait_send()
    go_east.wait_send()
    for copy in sent + more:
        copy.wait_send()
    for copy in stores:
        copy.wait()


def fused(nx, ny, forcing, damping, wind_lon, wind_lat, coup):
    rows = forcing.shape[1]
    total = rows + 2 * RIM
    vm = pl.BlockSpec(memory_space=pltpu.VMEM)
    hbm = pl.BlockSpec(memory_space=pltpu.HBM)
    dma = pltpu.SemaphoreType.DMA
    out = jax.ShapeDtypeStruct(forcing.shape, F32)
    return pl.pallas_call(
        functools.partial(kernel, nx, ny),
        out_shape=(out, out, jax.ShapeDtypeStruct((1, 1), F32)),
        in_specs=[hbm, hbm, hbm, hbm, vm, vm, hbm],
        out_specs=(hbm, hbm, pl.BlockSpec(memory_space=pltpu.SMEM)),
        scratch_shapes=[pltpu.VMEM((total, CH, 384), F32)] * ITERS + [
            pltpu.VMEM((total, 2 * CH, 384), F32),
            pltpu.VMEM((total, 8, 384), F32),
            pltpu.VMEM((total, CH, 384), F32),
            pltpu.VMEM((2, total, 384), F32),
            pltpu.VMEM((2, total // 8, 40, 128), F32),
            pltpu.VMEM((2, rows // 8, 40, 128), F32),
            pltpu.VMEM((total, 128), F32),
            pltpu.VMEM((2, 64, 384), F32),
            pltpu.VMEM((2, CH, 128), F32),
            pltpu.VMEM((2, CH, 128), F32),
            pltpu.VMEM((nx, 8, 128), F32),
            pltpu.VMEM((ny, 8, 128), F32),
            pltpu.VMEM((2, rows, CH, 256), F32),
            dma((2 * CH + 2,)), dma, dma((2,)), dma((2,)), dma((6,)), dma((6,)),
            dma((2,)), dma((2,)), dma((4,)), dma((4,)),
            dma((nx,)), dma((nx,)), dma((ny,)), dma((ny,)), dma((2, 2, CH)),
        ],
        compiler_params=pltpu.CompilerParams(
            collective_id=0, has_side_effects=True, vmem_limit_bytes=48 * 1024 * 1024),
        name="krylov",
    )(forcing, damping, wind_lon, wind_lat, coup,
      jnp.asarray(trial_table()), jnp.asarray(kx_table(rows * ny)))


def shifted(cells, axis, dim, closed, width):
    count = lax.axis_size(axis)
    ends = count if closed else count - 1
    head = lax.slice_in_dim(cells, 0, width, axis=dim)
    tail = lax.slice_in_dim(cells, cells.shape[dim] - width, cells.shape[dim], axis=dim)
    return jnp.concatenate(
        [
            lax.ppermute(tail, axis, [(i, (i + 1) % count) for i in range(ends)]),
            cells,
            lax.ppermute(head, axis, [((i + 1) % count, i) for i in range(ends)]),
        ],
        axis=dim,
    )


def apply_plain(vec, damping, coupling, wind_lon, wind_lat, kx):
    wide = shifted(vec, "gx", 2, True, 2)
    tall = shifted(vec, "gy", 1, False, 2)
    e1, w1, e2, w2 = wide[:, :, 3:-1], wide[:, :, 1:-3], wide[:, :, 4:], wide[:, :, :-4]
    n1, s1, n2, s2 = tall[:, 3:-1], tall[:, 1:-3], tall[:, 4:], tall[:, :-4]
    mixed = jnp.einsum("ij,jab->iab", coupling, vec, precision=lax.Precision.HIGHEST)
    return (
        (1.0 + damping) * vec + 0.25 * mixed
        + kx * (2.0 * vec - e1 - w1) + 0.5 * (2.0 * vec - n1 - s1)
        + wind_lon * ((8.0 * (e1 - w1) - (e2 - w2)) / 12.0)
        + wind_lat * ((8.0 * (n1 - s1) - (n2 - s2)) / 12.0)
    )


def careful(forcing, damping, coupling, wind_lon, wind_lat):
    rows = forcing.shape[1]
    pos = (lax.axis_index("gy") * rows + jnp.arange(rows)).astype(F32)
    phi = -math.pi / 2 + (pos + 0.5) * (math.pi / (rows * lax.axis_size("gy")))
    kx = (0.5 / (jnp.cos(phi) ** 2 + 0.1))[:, None]
    operate = lambda v: apply_plain(v, damping, coupling, wind_lon, wind_lat, kx)
    every = ("gx", "gy")
    first = jnp.sqrt(lax.psum(jnp.sum(forcing * forcing), every) + 1.0)
    basis = jnp.zeros((ITERS,) + forcing.shape, F32).at[0].set(forcing / first)
    heights = jnp.zeros((ITERS + 1, ITERS), F32)

    def body(j, state):
        basis, heights = state
        w = operate(lax.dynamic_index_in_dim(basis, j, 0, keepdims=False))
        h = lax.psum(jnp.sum(basis * w[None], axis=(1, 2, 3)), every)
        w = w - jnp.sum(h[:, None, None, None] * basis, axis=0)
        below = jnp.sqrt(lax.psum(jnp.sum(w * w), every) + 1.0)
        col = jnp.concatenate([h, jnp.zeros((1,), F32)])
        col = jnp.where(jnp.arange(ITERS + 1) == j + 1, below, col)
        heights = lax.dynamic_update_slice(heights, col[:, None], (0, j))
        old = lax.dynamic_index_in_dim(basis, jnp.minimum(j + 1, ITERS - 1), 0, keepdims=False)
        new = jnp.where(j + 1 < ITERS, w / below, old)
        basis = lax.dynamic_update_index_in_dim(basis, new, jnp.minimum(j + 1, ITERS - 1), 0)
        return basis, heights

    basis, heights = lax.fori_loop(0, ITERS, body, (basis, heights))
    h = [[heights[i, j] for j in range(ITERS)] for i in range(ITERS + 1)]
    target = [first] + [jnp.zeros((), F32)] * ITERS
    turns = []
    for j in range(ITERS):
        for i in range(j):
            c, s = turns[i]
            h[i][j], h[i + 1][j] = c * h[i][j] + s * h[i + 1][j], c * h[i + 1][j] - s * h[i][j]
        radius = jnp.sqrt(h[j][j] * h[j][j] + h[j + 1][j] * h[j + 1][j])
        c, s = h[j][j] / radius, h[j + 1][j] / radius
        turns.append((c, s))
        h[j][j] = radius
        target[j], target[j + 1] = c * target[j] + s * target[j + 1], c * target[j + 1] - s * target[j]
    y = [None] * ITERS
    for j in reversed(range(ITERS)):
        part = target[j]
        for i in range(j + 1, ITERS):
            part = part - h[j][i] * y[i]
        y[j] = part / h[j][j]
    weights = jnp.stack(y)
    answer = jnp.sum(weights[:, None, None, None] * basis, axis=0)
    return answer, forcing - operate(answer)


def per_device(nx, ny, forcing, damping, coupling, wind_lon, wind_lat):
    sol, res, flag = fused(nx, ny, forcing, damping, wind_lon, wind_lat, coupling)

    pin = lambda x: with_layout_constraint(x, Layout(tuple(range(x.ndim))))

    def again(state):
        sol, res = careful(pin(forcing), pin(damping), coupling, wind_lon, wind_lat)
        return pin(sol), pin(res), jnp.zeros((), F32)

    done = lax.while_loop(lambda state: state[2] > 0.5, again, (sol, res, flag[0, 0]))
    return pin(done[0]), pin(done[1])


def solution(mesh):
    nx, ny = mesh.shape["gx"], mesh.shape["gy"]
    in_specs = (P(None, "gy", "gx"), P(None, "gy", "gx"), P(), P("gy", "gx"), P("gy", "gx"))
    out_specs = (P(None, "gy", "gx"), P(None, "gy", "gx"))
    return jax.shard_map(
        functools.partial(per_device, nx, ny),
        mesh=mesh, in_specs=in_specs, out_specs=out_specs, check_vma=False,
    )
```

time: 69.4 us -> 49.2 us (0.71)
  Pallas kernels: 53.3 us -> 41.3 us
  local copies, waits for them, and re-layouts: 13 us -> 5.59 us
  between operations: 1.41 us -> 0.66 us
    pallas_call x1, Pallas kernels: 53.3 us -> 41.3 us  [fused(): pl.pallas_call(functools.partial(kernel, nx, ny), out_shape=(out, out, ja...]
    cond x2 -> x0, local copies, waits for them, and re-layouts: 3.68 us -> none  [per_device(): return lax.cond(trusted, back, slow)]
    broadcast_in_dim x3 -> x0, local copies, waits for them, and re-layouts: 2.8 us -> none  [the longest x1 1.39 us: per_device(): wind_lon[None]]
    concatenate x1 -> x0, local copies, waits for them, and re-layouts: 2.09 us -> none  [per_device(): jnp.concatenate([forcing, damping, wind_lon[None], wind_lat[None], pad],...]
    unnamed x17 -> x6, local copies, waits for them, and re-layouts: 4.44 us -> 5.59 us
where the time goes in v2:
time: 49.2 us; the launch traced here: 48.3 us
  Pallas kernels  41.3 us (84%)
  local copies, waits for them, and re-layouts  5.59 us (11%)
  loops' own time  0.81 us (2%)
  between operations  0.66 us (1%)
    pallas_call x1, Pallas kernels, fused(): pl.pallas_call(functools.partial(kernel, nx, ny), out_shape=(out, out, ja...  41.3 us
    unnamed x6, local copies, waits for them, and re-layouts  5.59 us

profile of v2, /device:TPU:0, one launch (start us, length us, event | category | flops | bytes accessed | tf_op | source)
XLA Modules:
  0.0 48.3 jit_solution(741477960004047772)
XLA Ops:
  0.6 0.0 copy-start
  0.6 0.9 %copy-done = f32[528,128]{1,0:T(8,128)S(1)} copy-done((f32[528,128]{1,0:T(8,128)S(1)}, f32[528,128]{1,0:T(8,128)}, u32[]{:S(2)}) %copy-start) | copy-done | bytes 270360
  1.6 0.0 copy-start.1
  1.6 0.9 %copy-done.1 = f32[9,16,128]{2,1,0:T(8,128)S(1)} copy-done((f32[9,16,128]{2,1,0:T(8,128)S(1)}, f32[9,16,128]{2,1,0:T(8,128)}, u32[]{:S(2)}) %copy-start.1) | copy-done | bytes 73752
  2.5 41.3 %krylov.1 = (f32[16,32,256]{2,1,0:T(8,128)}, f32[16,32,256]{2,1,0:T(8,128)}, f32[1,1]{1,0:T(1,128)}) custom-call(f32[16,32,256]{2,1,0:T(8,128)} %forc.1, f32[16,32,256]{2,1,0:T(8,128)} %damp.1, f32[32,256]{1,0:T(8,128)} %wlon.1, f32[32,256]{1,0:T(8,128)} %wlat.1, f32[16,16]{1,0:T(8,128)} %coup.1, f32[9,16,128]{2,1,0:T(8,128)S(1)} %copy-done.1, ...), custom_call_target="tpu_custom_call" | custom-call | tf_op jit(solution)/shard_map/krylov/pallas_call | solution.py:534
  43.7 0.8 %while.26 = (f32[16,32,256]{2,1,0:T(8,128)}, f32[16,32,256]{2,1,0:T(8,128)}, f32[]{:T(128)}, f32[16,32,256]{2,1,0:T(8,128)}, f32[16,32,256]{2,1,0:T(8,128)}, /*i...) while((f32[16,32,256]{2,1,0:T(8,128)}, f32[16,32,256]{2,1,0:T(8,128)}, f32[]{:T(128)}, ...), condition=%region_11.12_spmd, body=%region_0.11_spmd | while | flops 65700388 | bytes 64118152 | solution.py:651
  44.6 1.9 %copy.58 = f32[16,32,256]{2,1,0:T(8,128)} copy(f32[16,32,256]{2,1,0:T(8,128)} %get-tuple-element.476) | data formatting | bytes 1048576
  46.4 1.9 %copy.59 = f32[16,32,256]{2,1,0:T(8,128)} copy(f32[16,32,256]{2,1,0:T(8,128)} %get-tuple-element.477) | data formatting | bytes 1048576
Async XLA Ops:
  0.6 1.0 %copy-start = (f32[528,128]{1,0:T(8,128)S(1)}, f32[528,128]{1,0:T(8,128)}, u32[]{:S(2)}) copy-start(f32[528,128]{1,0:T(8,128)} %constant.161.clone.kxs) | copy-start | bytes 811012
  1.6 0.9 %copy-start.1 = (f32[9,16,128]{2,1,0:T(8,128)S(1)}, f32[9,16,128]{2,1,0:T(8,128)}, u32[]{:S(2)}) copy-start(f32[9,16,128]{2,1,0:T(8,128)} %constant.160.clone.trial) | copy-start | bytes 221188

commit v3 on v2

--- a/solution.py
+++ b/solution.py
@@ -22,24 +22,26 @@
 F32 = jnp.float32
 
 
-def trial_table():
-    rng = np.random.default_rng(7)
-    draw = rng.choice([-1.0, 1.0], size=(9, 16, 128)) * NOISE
-    table = np.zeros((9, 16, 128), np.float32)
-    for i in range(9):
-        for k in range(i, 9):
-            table[i, k] = draw[i, k]
-            table[k, i] = draw[i, k]
-    table[:, :, 0] = 0.0
-    return table
-
-
-def kx_table(lat_total):
-    row = np.arange(lat_total) + 0.5
-    phi = -math.pi / 2 + row * (math.pi / lat_total)
-    table = np.zeros((lat_total + 2 * RIM, 128), np.float32)
-    table[RIM : RIM + lat_total] = (0.5 / (np.cos(phi) ** 2 + 0.1))[:, None]
-    return table
+def trials():
+    sub = lax.broadcasted_iota(jnp.int32, (16, 128), 0)
+    lane = lanes((16, 128))
+    tables = []
+    for k in range(9):
+        pair = jnp.minimum(sub, k) * 16 + jnp.maximum(sub, k)
+        bits = pair * 1640531527 + lane * 668265263
+        bits = (bits ^ lax.shift_right_logical(bits, 15)) * 739982445
+        bits = bits ^ lax.shift_right_logical(bits, 13)
+        sign = jnp.where((bits & 64) == 0, NOISE, -NOISE)
+        tables.append(jnp.where((lane == 0) | (sub > 8), 0.0, sign))
+    return tables
+
+
+def row_kx(first, count, lat_total):
+    row = (first + lax.broadcasted_iota(jnp.int32, (count, 128), 0)).astype(F32)
+    phi = -math.pi / 2 + (row + 0.5) * (math.pi / lat_total)
+    inside = (row >= 0.0) & (row < lat_total)
+    cos = jnp.cos(phi)
+    return jnp.where(inside, 0.5 / (cos * cos + 0.1), 0.0)
 
 
 def lanes(shape):
@@ -107,13 +109,13 @@
 
 
 def kernel(
-    nx, ny, forc, damp, wlon, wlat, coup, trial, kxs, sol, res, flag,
+    nx, ny, forc, damp, wlon, wlat, coup_hbm, outs, flag,
     *scratch,
 ):
     pwr, scratch = scratch[:ITERS], scratch[ITERS:]
-    (ext, coef, main, wind, lon, pack, kxv, mix, made, rims, gx_slots, gy_slots, outs,
-     in_sem, kx_sem, lon_send, lon_recv, lat_send, lat_recv, cor_send, cor_recv,
-     mid_send, mid_recv, gxs_send, gxs_recv, gys_send, gys_recv, out_sem) = scratch
+    (ext, coef, main, wind, lon, pack, kxv, coup, made, rims, gx_slots, gy_slots,
+     in_sem, lon_send, lon_recv, lat_send, lat_recv, cor_send, cor_recv,
+     mid_send, mid_recv, gxs_send, gxs_recv, gys_send, gys_recv) = scratch
     gx, gy = lax.axis_index("gx"), lax.axis_index("gy")
     rows = forc.shape[1]
     top = RIM + rows
@@ -133,8 +135,7 @@
     for n, src in enumerate((wlon, wlat)):
         loads.append(pltpu.make_async_copy(
             src, wind.at[n, pl.ds(RIM, rows), pl.ds(0, 256)], in_sem.at[2 * CH + n]))
-    start = pl.multiple_of(gy * rows, 8)
-    loads.append(pltpu.make_async_copy(kxs.at[pl.ds(start, total), :], kxv, kx_sem))
+    loads.append(pltpu.make_async_copy(coup_hbm, coup, in_sem.at[2 * CH + 2]))
     for copy in loads:
         copy.start()
 
@@ -143,8 +144,45 @@
         pl.semaphore_signal(barrier, 1, device_id=(lax.rem(gx + k, nx), gy), device_id_type=MESH)
     for k in range(1, ny):
         pl.semaphore_signal(barrier, 1, device_id=(gx, lax.rem(gy + k, ny)), device_id_type=MESH)
+    kxv[...] = row_kx(gy * rows - RIM, total, rows * ny)
     for copy in loads:
         copy.wait()
+
+    pl.semaphore_wait(barrier, nx + ny - 2)
+
+    def strip(ref, src, dst, size, chan, sem, peer):
+        return pltpu.make_async_remote_copy(
+            ref.at[pl.ds(src, size), chan, pl.ds(0, 256)],
+            ref.at[pl.ds(dst, size), chan, pl.ds(0, 256)],
+            lat_send.at[sem], lat_recv.at[sem], device_id=(gx, peer), device_id_type=MESH)
+
+    def breeze(src, dst, sem, peer):
+        return pltpu.make_async_remote_copy(
+            wind.at[:, pl.ds(src, 8), pl.ds(0, 256)], wind.at[:, pl.ds(dst, 8), pl.ds(0, 256)],
+            lat_send.at[sem], lat_recv.at[sem], device_id=(gx, peer), device_id_type=MESH)
+
+    vec, par = pl.ds(0, CH), pl.ds(CH, CH)
+    to_s = [breeze(RIM, top, 4, south), strip(ext, RIM, top, RIM, vec, 0, south),
+            strip(ext, RIM, top, RIM - 2, par, 1, south)]
+    to_n = [breeze(rows, 0, 5, north), strip(ext, rows, 0, RIM, vec, 2, north),
+            strip(ext, rows + 2, 2, RIM - 2, par, 3, north)]
+
+    @pl.when(has_s)
+    def _():
+        for copy in to_s:
+            copy.start()
+
+    @pl.when(has_n)
+    def _():
+        for copy in to_n:
+            copy.start()
+
+    for missing, row, slot in ((no_s, 0, 0), (no_n, top, groups + 1)):
+        @pl.when(missing)
+        def _():
+            ext[row : row + RIM, 0 : 2 * CH, 0:256] = jnp.zeros((RIM, 2 * CH, 256), F32)
+            wind[:, row : row + RIM, 0:256] = jnp.zeros((2, RIM, 256), F32)
+            lon[:, slot] = jnp.zeros((2, 40, 128), F32)
 
     def turn(value, by):
         by = by % 128
@@ -166,8 +204,6 @@
             b = turn(wind[1, at, cut], 16 + shift)
             pack[side, g, 2 * CH :, :] = jnp.where(lane8 < 16, a, b)
 
-    pl.semaphore_wait(barrier, nx + ny - 2)
-
     go_west = pltpu.make_async_remote_copy(
         pack.at[0], lon.at[0, pl.ds(1, groups)], lon_send.at[0], lon_recv.at[0],
         device_id=(west, gy), device_id_type=MESH)
@@ -176,40 +212,6 @@
         device_id=(east, gy), device_id_type=MESH)
     go_west.start()
     go_east.start()
-
-    def strip(ref, src, dst, size, chan, sem, peer):
-        return pltpu.make_async_remote_copy(
-            ref.at[pl.ds(src, size), chan, pl.ds(0, 256)],
-            ref.at[pl.ds(dst, size), chan, pl.ds(0, 256)],
-            lat_send.at[sem], lat_recv.at[sem], device_id=(gx, peer), device_id_type=MESH)
-
-    def breeze(src, dst, sem, peer):
-        return pltpu.make_async_remote_copy(
-            wind.at[:, pl.ds(src, 8), pl.ds(0, 256)], wind.at[:, pl.ds(dst, 8), pl.ds(0, 256)],
-            lat_send.at[sem], lat_recv.at[sem], device_id=(gx, peer), device_id_type=MESH)
-
-    vec, par = pl.ds(0, CH), pl.ds(CH, CH)
-    to_s = [breeze(RIM, top, 4, south), strip(ext, RIM, top, RIM, vec, 0, south),
-            strip(ext, RIM, top, RIM - 2, par, 1, south)]
-    to_n = [breeze(rows, 0, 5, north), strip(ext, rows, 0, RIM, vec, 2, north),
-            strip(ext, rows + 2, 2, RIM - 2, par, 3, north)]
-
-    @pl.when(has_s)
-    def _():
-        for copy in to_s:
-            copy.start()
-
-    @pl.when(has_n)
-    def _():
-        for copy in to_n:
-            copy.start()
-
-    for missing, row, slot in ((no_s, 0, 0), (no_n, top, groups + 1)):
-        @pl.when(missing)
-        def _():
-            ext[row : row + RIM, 0 : 2 * CH, 0:256] = jnp.zeros((RIM, 2 * CH, 256), F32)
-            wind[:, row : row + RIM, 0:256] = jnp.zeros((2, RIM, 256), F32)
-            lon[:, slot] = jnp.zeros((2, 40, 128), F32)
 
     go_west.wait_recv()
     go_east.wait_recv()
@@ -314,17 +316,8 @@
 
     def inner(k):
         m = k % BLOCK + 1
-        low, count = RIM + 2 * m, (rows - 4 * m) // 4
-        mix[0] = couple(power(k), low)
-
-        def body(g, carry):
-            r0 = low + 4 * g
-            ahead = couple(power(k), jnp.minimum(r0 + 4, low + 4 * (count - 1)))
-            stencil(k, r0, mix[g % 2])
-            mix[(g + 1) % 2] = ahead
-            return carry
-
-        lax.fori_loop(0, count, body, 0)
+        for r0 in range(RIM + 2 * m, top - 2 * m, 4):
+            stencil(k, r0, couple(power(k), r0))
 
     def outer(k):
         m = k % BLOCK + 1
@@ -436,7 +429,7 @@
     sums = dict(zip(pairs, sums))
     folded = {p: jnp.sum(s, axis=0, keepdims=True) for p, s in sums.items()}
     sub8 = lax.broadcasted_iota(jnp.int32, (8, 128), 0)
-    mine = jnp.zeros((8, 128), F32)
+    spread = jnp.zeros((8, 128), F32)
     for k in range(10):
         col = jnp.zeros((8, 128), F32)
         if k < 9:
@@ -444,7 +437,9 @@
                 col = jnp.where(sub8 == i, folded[min(i, k), max(i, k)], col)
         else:
             col = jnp.where(sub8 == 0, folded[8, 8], col)
-        mine = jnp.where(lane8 == k, jnp.sum(col, axis=1, keepdims=True), mine)
+        total_k = jnp.sum(col, axis=1, keepdims=True)
+        spread = jnp.where(lane8 == 8 * k + sub8, total_k, spread)
+    mine = jnp.sum(spread, axis=0, keepdims=True)
 
     def reduce_over(value, slots, send, recv, me, count, device):
         slots[me] = value
@@ -469,7 +464,9 @@
     value, sent = reduce_over(mine, gx_slots, gxs_send, gxs_recv, gx, nx, lambda p: (p, gy))
     value, more = reduce_over(value, gy_slots, gys_send, gys_recv, gy, ny, lambda p: (gx, p))
 
-    upper = [jnp.broadcast_to(value[:, k : k + 1], (8, 128)) for k in range(10)]
+    value = jnp.broadcast_to(value, (8, 128))
+    picked = [jnp.where(lane8 == 8 * k + sub8, value, 0.0) for k in range(10)]
+    upper = [jnp.broadcast_to(jnp.sum(p, axis=1, keepdims=True), (8, 128)) for p in picked]
     lower = [upper[8][k : k + 1, :] for k in range(8)] + [upper[9][0:1, :]]
     plain = [jnp.concatenate([u, jnp.where(sub8 == 0, w, 0.0)]) for u, w in zip(upper, lower)]
     sub = lax.broadcasted_iota(jnp.int32, (16, 128), 0)
@@ -477,6 +474,7 @@
     for k in range(9):
         diag = jnp.where(sub == k, plain[k], diag)
     size = jnp.sqrt(diag)
+    trial = trials()
     cols = [plain[k] + trial[k] * size * size[k : k + 1, :] for k in range(9)]
     q = gmres(cols)
     d = apply_a(q)
@@ -491,36 +489,35 @@
 
     qs = [q0[k : k + 1, :] for k in range(8)]
     ds = [left0[k : k + 1, :] for k in range(9)]
-    stores = []
-    part = rows // 2
-    for h in range(2):
-        @pl.loop(h * part, (h + 1) * part)
-        def _(r):
-            for t in range(2):
-                cut = pl.ds(128 * t, 128)
-                vals = [power(k)[r + RIM, :, cut] for k in range(9)]
-                s = qs[0] * vals[0]
-                e = ds[0] * vals[0]
-                for k in range(1, 8):
-                    s = s + qs[k] * vals[k]
-                for k in range(1, 9):
-                    e = e + ds[k] * vals[k]
-                outs[0, r, :, cut] = s
-                outs[1, r, :, cut] = e
-
-        for c in range(CH):
-            for n, dst in enumerate((sol, res)):
-                copy = pltpu.make_async_copy(
-                    outs.at[n, pl.ds(h * part, part), c, :],
-                    dst.at[c, pl.ds(h * part, part), :], out_sem.at[h, n, c])
-                copy.start()
-                stores.append(copy)
+
+    @pl.loop(0, rows)
+    def _(r):
+        for t in range(2):
+            cut = pl.ds(128 * t, 128)
+            vals = [power(k)[r + RIM, :, cut] for k in range(9)]
+            s = qs[0] * vals[0]
+            e = ds[0] * vals[0]
+            for k in range(1, 8):
+                s = s + qs[k] * vals[k]
+            for k in range(1, 9):
+                e = e + ds[k] * vals[k]
+            outs[0, r, :, cut] = s
+            outs[1, r, :, cut] = e
 
     go_west.wait_send()
     go_east.wait_send()
     for copy in sent + more:
         copy.wait_send()
-    for copy in stores:
+
+
+def unfold(outs, sol, res, sem):
+    copies = []
+    for c in range(CH):
+        for n, dst in enumerate((sol, res)):
+            copies.append(pltpu.make_async_copy(outs.at[n, :, c, :], dst.at[c], sem.at[n, c]))
+    for copy in copies:
+        copy.start()
+    for copy in copies:
         copy.wait()
 
 
@@ -530,12 +527,11 @@
     vm = pl.BlockSpec(memory_space=pltpu.VMEM)
     hbm = pl.BlockSpec(memory_space=pltpu.HBM)
     dma = pltpu.SemaphoreType.DMA
-    out = jax.ShapeDtypeStruct(forcing.shape, F32)
-    return pl.pallas_call(
+    outs, flag = pl.pallas_call(
         functools.partial(kernel, nx, ny),
-        out_shape=(out, out, jax.ShapeDtypeStruct((1, 1), F32)),
-        in_specs=[hbm, hbm, hbm, hbm, vm, vm, hbm],
-        out_specs=(hbm, hbm, pl.BlockSpec(memory_space=pltpu.SMEM)),
+        out_shape=(jax.ShapeDtypeStruct((2, rows, CH, 256), F32), jax.ShapeDtypeStruct((1, 1), F32)),
+        in_specs=[hbm] * 5,
+        out_specs=(vm, pl.BlockSpec(memory_space=pltpu.SMEM)),
         scratch_shapes=[pltpu.VMEM((total, CH, 384), F32)] * ITERS + [
             pltpu.VMEM((total, 2 * CH, 384), F32),
             pltpu.VMEM((total, 8, 384), F32),
@@ -544,21 +540,30 @@
             pltpu.VMEM((2, total // 8, 40, 128), F32),
             pltpu.VMEM((2, rows // 8, 40, 128), F32),
             pltpu.VMEM((total, 128), F32),
-            pltpu.VMEM((2, 64, 384), F32),
+            pltpu.VMEM((CH, CH), F32),
             pltpu.VMEM((2, CH, 128), F32),
             pltpu.VMEM((2, CH, 128), F32),
-            pltpu.VMEM((nx, 8, 128), F32),
-            pltpu.VMEM((ny, 8, 128), F32),
-            pltpu.VMEM((2, rows, CH, 256), F32),
-            dma((2 * CH + 2,)), dma, dma((2,)), dma((2,)), dma((6,)), dma((6,)),
+            pltpu.VMEM((nx, 1, 128), F32),
+            pltpu.VMEM((ny, 1, 128), F32),
+            dma((2 * CH + 3,)), dma((2,)), dma((2,)), dma((6,)), dma((6,)),
             dma((2,)), dma((2,)), dma((4,)), dma((4,)),
-            dma((nx,)), dma((nx,)), dma((ny,)), dma((ny,)), dma((2, 2, CH)),
+            dma((nx,)), dma((nx,)), dma((ny,)), dma((ny,)),
         ],
         compiler_params=pltpu.CompilerParams(
             collective_id=0, has_side_effects=True, vmem_limit_bytes=48 * 1024 * 1024),
         name="krylov",
-    )(forcing, damping, wind_lon, wind_lat, coup,
-      jnp.asarray(trial_table()), jnp.asarray(kx_table(rows * ny)))
+    )(forcing, damping, wind_lon, wind_lat, coup)
+    field = jax.ShapeDtypeStruct(forcing.shape, F32)
+    sol, res = pl.pallas_call(
+        unfold,
+        out_shape=(field, field),
+        in_specs=[vm],
+        out_specs=(hbm, hbm),
+        scratch_shapes=[dma((2, CH))],
+        compiler_params=pltpu.CompilerParams(vmem_limit_bytes=8 * 1024 * 1024),
+        name="unfold",
+    )(outs)
+    return sol, res, flag
 
 
 def shifted(cells, axis, dim, closed, width):

time: 49.2 us -> 41.2 us (0.84); the launches traced: 48.3 us -> 40.9 us
  local copies, waits for them, and re-layouts: 5.59 us -> 0 us
  Pallas kernels: 41.3 us -> 39.3 us
    unnamed x6 -> x0, local copies, waits for them, and re-layouts: 5.59 us -> none
    pallas_call x1 -> x2, Pallas kernels: 41.3 us -> 39.3 us  [the longest x1 38 us: fused(): pl.pallas_call(functools.partial(kernel, nx, ny), out_shape=(jax.ShapeDty...]
where the time goes in v3:
time: 41.2 us; the launch traced here: 40.9 us
  Pallas kernels  39.3 us (95%)
  loops' own time  0.84 us (2%)
  between operations  0.83 us (2%)
    pallas_call x1, Pallas kernels, fused(): pl.pallas_call(functools.partial(kernel, nx, ny), out_shape=(jax.ShapeDty...  38 us
    pallas_call x1, Pallas kernels, fused(): pl.pallas_call(unfold, out_shape=(field, field), in_specs=[vm], out_specs...  1.23 us
    another operation x1, loops' own time, per_device(): lax.while_loop(lambda state: state[2] > 0.5, again, (sol, res, flag[0, 0]))  0.84 us

profile of v3, /device:TPU:0, one launch (start us, length us, event | category | flops | bytes accessed | tf_op | source)
XLA Modules:
  0.0 40.9 jit_solution(9560053414699581519)
XLA Ops:
  0.6 38.0 %krylov.1 = (f32[2,32,16,256]{3,2,1,0:T(8,128)S(1)}, f32[1,1]{1,0:T(1,128)}) custom-call(f32[16,32,256]{2,1,0:T(8,128)} %forc.1, f32[16,32,256]{2,1,0:T(8,128)} %damp.1, f32[32,256]{1,0:T(8,128)} %wlon.1, f32[32,256]{1,0:T(8,128)} %wlat.1, f32[16,16]{1,0:T(8,128)} %coup_hbm.1), custom_call_target="tpu_custom_call" | custom-call | tf_op jit(solution)/shard_map/krylov/pallas_call | solution.py:530
  38.7 1.2 %unfold.1 = (f32[16,32,256]{2,1,0:T(8,128)}, f32[16,32,256]{2,1,0:T(8,128)}) custom-call(f32[2,32,16,256]{3,2,1,0:T(8,128)S(1)} %get-tuple-element.198.outs), custom_call_target="tpu_custom_call" | custom-call | tf_op jit(solution)/shard_map/unfold/pallas_call | solution.py:557
  39.9 0.8 %while.26 = (f32[16,32,256]{2,1,0:T(8,128)}, f32[16,32,256]{2,1,0:T(8,128)}, f32[]{:T(128)}, f32[16,32,256]{2,1,0:T(8,128)}, f32[16,32,256]{2,1,0:T(8,128)}, /*i...) while((f32[16,32,256]{2,1,0:T(8,128)}, f32[16,32,256]{2,1,0:T(8,128)}, f32[]{:T(128)}, ...), condition=%region_11.12_spmd, body=%region_0.11_spmd | while | flops 65700388 | bytes 64118152 | solution.py:656

commit v4 on v3

--- a/solution.py
+++ b/solution.py
@@ -126,6 +126,19 @@
     has_n, has_s = gy < ny - 1, gy > 0
     no_n, no_s = jnp.logical_not(has_n), jnp.logical_not(has_s)
 
+    core, place = lax.rem(gx, 2), gx // 2
+    half_x = nx // 2
+    team = half_x * ny
+    hops = [(a, b) for a in range(half_x) for b in range(ny) if (a, b) != (0, 0)]
+    hops.sort(key=lambda h: min(h[0], half_x - h[0]) + min(h[1], ny - h[1]))
+
+    def mate(a, b):
+        return (2 * lax.rem(place + a, half_x) + core, lax.rem(gy + b, ny))
+
+    barrier = pltpu.get_barrier_semaphore()
+    for peer in [(east, gy), (west, gy)] + [mate(a, b) for a, b in hops]:
+        pl.semaphore_signal(barrier, 1, device_id=peer, device_id_type=MESH)
+
     loads = []
     for c in range(CH):
         for n, src in enumerate((forc, damp)):
@@ -139,16 +152,11 @@
     for copy in loads:
         copy.start()
 
-    barrier = pltpu.get_barrier_semaphore()
-    for k in range(1, nx):
-        pl.semaphore_signal(barrier, 1, device_id=(lax.rem(gx + k, nx), gy), device_id_type=MESH)
-    for k in range(1, ny):
-        pl.semaphore_signal(barrier, 1, device_id=(gx, lax.rem(gy + k, ny)), device_id_type=MESH)
     kxv[...] = row_kx(gy * rows - RIM, total, rows * ny)
     for copy in loads:
         copy.wait()
 
-    pl.semaphore_wait(barrier, nx + ny - 2)
+    pl.semaphore_wait(barrier, team + 1)
 
     def strip(ref, src, dst, size, chan, sem, peer):
         return pltpu.make_async_remote_copy(
@@ -162,10 +170,36 @@
             lat_send.at[sem], lat_recv.at[sem], device_id=(gx, peer), device_id_type=MESH)
 
     vec, par = pl.ds(0, CH), pl.ds(CH, CH)
-    to_s = [breeze(RIM, top, 4, south), strip(ext, RIM, top, RIM, vec, 0, south),
-            strip(ext, RIM, top, RIM - 2, par, 1, south)]
-    to_n = [breeze(rows, 0, 5, north), strip(ext, rows, 0, RIM, vec, 2, north),
-            strip(ext, rows + 2, 2, RIM - 2, par, 3, north)]
+    near_s = [breeze(RIM, top, 0, south), strip(ext, RIM, top, 4, vec, 1, south),
+              strip(ext, RIM, top, 4, par, 2, south)]
+    far_s = [strip(ext, RIM + 4, top + 4, 4, vec, 3, south),
+             strip(ext, RIM + 4, top + 4, 2, par, 4, south)]
+    near_n = [breeze(rows, 0, 5, north), strip(ext, rows + 4, 4, 4, vec, 6, north),
+              strip(ext, rows + 4, 4, 4, par, 7, north)]
+    far_n = [strip(ext, rows, 0, 4, vec, 8, north), strip(ext, rows + 2, 2, 2, par, 9, north)]
+    to_s, to_n = near_s + far_s, near_n + far_n
+
+    def await_strips(from_s, from_n):
+        @pl.when(has_s)
+        def _():
+            for copy in from_s:
+                copy.wait_recv()
+
+        @pl.when(has_n)
+        def _():
+            for copy in from_n:
+                copy.wait_recv()
+
+    def await_sent(gone_s, gone_n):
+        @pl.when(has_s)
+        def _():
+            for copy in gone_s:
+                copy.wait_send()
+
+        @pl.when(has_n)
+        def _():
+            for copy in gone_n:
+                copy.wait_send()
 
     @pl.when(has_s)
     def _():
@@ -244,7 +278,7 @@
         at = lanes(from_e.shape)
         return jnp.where(at < 16, from_e, jnp.where(at >= 112, from_w, 0.0))
 
-    def prepare(g):
+    def third(g):
         at = pl.ds(pl.multiple_of(8 * g, 8), 8)
         for j in range(8):
             ext[8 * g + j, 0 : 2 * CH, 256:384] = merge(
@@ -252,12 +286,15 @@
         for n in range(2):
             wind[n, at, 256:384] = merge(
                 turn(lon[0, g, 2 * CH :, :], -16 * n), turn(lon[1, g, 2 * CH :, :], 112 - 16 * n))
+
+    def prepare(g, some=range(8)):
+        at = pl.ds(pl.multiple_of(8 * g, 8), 8)
         kx8 = kxv[at, :]
         in8 = jnp.where(kx8 > 0.0, 1.0, 0.0)
         for t in range(3):
             cut = pl.ds(128 * t, 128)
             lon8, lat8 = wind[0, at, cut], wind[1, at, cut]
-            for j in range(8):
+            for j in some:
                 one = slice(j, j + 1)
                 coef[8 * g + j, :, cut] = (
                     kx8[one] * by_kx + in8[one] * by_one + by_lon * lon8[one] + by_lat * lat8[one])
@@ -267,6 +304,7 @@
 
     @pl.loop(1, groups + 1)
     def _(g):
+        third(g)
         prepare(g)
 
     cm = coup[...] * (0.25 * two)
@@ -319,36 +357,26 @@
         for r0 in range(RIM + 2 * m, top - 2 * m, 4):
             stencil(k, r0, couple(power(k), r0))
 
-    def outer(k):
+    def outer(k, far):
         m = k % BLOCK + 1
-        for r0 in (2 * m, 2 * m + 4, top - 2 * m, top - 2 * m + 4):
+        for r0 in ((2 * m, top - 2 * m + 4) if far else (2 * m + 4, top - 2 * m)):
             stencil(k, r0, couple(power(k), r0))
 
     for k in range(BLOCK):
         inner(k)
 
-    @pl.when(has_s)
-    def _():
-        for copy in to_s:
-            copy.wait_send()
-        cor_s.wait_send()
-        for copy in to_n:
-            copy.wait_recv()
-        cor_n.wait_recv()
-
-    @pl.when(has_n)
-    def _():
-        for copy in to_n:
-            copy.wait_send()
-        cor_n.wait_send()
-        for copy in to_s:
-            copy.wait_recv()
-        cor_s.wait_recv()
-
-    prepare(0)
-    prepare(groups + 1)
+    await_strips(near_n + [cor_n], near_s + [cor_s])
+    third(0)
+    third(groups + 1)
+    prepare(0, range(4, 8))
+    prepare(groups + 1, range(4))
     for k in range(BLOCK):
-        outer(k)
+        outer(k, False)
+    await_strips(far_n, far_s)
+    prepare(0, range(2, 4))
+    prepare(groups + 1, range(4, 6))
+    for k in range(BLOCK):
+        outer(k, True)
 
     half = power(BLOCK)
     lane16 = lanes((CH, 128))
@@ -361,7 +389,7 @@
 
     def again(src, dst, sem, peer):
         return pltpu.make_async_remote_copy(
-            half.at[pl.ds(src, RIM), :, pl.ds(0, 256)], half.at[pl.ds(dst, RIM), :, pl.ds(0, 256)],
+            half.at[pl.ds(src, 4), :, pl.ds(0, 256)], half.at[pl.ds(dst, 4), :, pl.ds(0, 256)],
             mid_send.at[sem], mid_recv.at[sem], device_id=(gx, peer), device_id_type=MESH)
 
     def also(src, dst, sem, peer):
@@ -369,8 +397,11 @@
             made.at[src], rims.at[dst], mid_send.at[sem], mid_recv.at[sem],
             device_id=(gx, peer), device_id_type=MESH)
 
-    mid_s = [also(0, 1, 2, south), again(RIM, top, 0, south)]
-    mid_n = [also(1, 0, 3, north), again(rows, 0, 1, north)]
+    near_s = [also(0, 1, 0, south), again(RIM, top, 1, south)]
+    far_s2 = [again(RIM + 4, top + 4, 2, south)]
+    near_n = [also(1, 0, 3, north), again(rows + 4, 4, 4, north)]
+    far_n2 = [again(rows, 0, 5, north)]
+    mid_s, mid_n = near_s + far_s2, near_n + far_n2
 
     @pl.when(has_s)
     def _():
@@ -403,28 +434,18 @@
 
     sums = tuple(jnp.zeros((8, 128), F32) for _ in pairs)
     sums = lax.fori_loop(2 * RIM, top - RIM, gram, sums)
-
-    @pl.when(has_s)
-    def _():
-        for copy in mid_s:
-            copy.wait_send()
-        for copy in mid_n:
-            copy.wait_recv()
-
-    @pl.when(has_n)
-    def _():
-        for copy in mid_n:
-            copy.wait_send()
-        for copy in mid_s:
-            copy.wait_recv()
-
+    await_strips(near_n, near_s)
     for side, row in ((0, 0), (1, top)):
         for j in range(8):
             half[row + j, :, 256:384] = turn(rims[side], -16 * j - 8)
     for k in range(BLOCK, ITERS):
-        outer(k)
-    sums = lax.fori_loop(RIM, 2 * RIM, gram, sums)
-    sums = lax.fori_loop(top - RIM, top, gram, sums)
+        outer(k, False)
+    sums = lax.fori_loop(
+        0, 8, lambda g, acc: gram(RIM + 4 + g + (rows - 16) * (g // 4), acc), sums)
+    await_strips(far_n2, far_s2)
+    for k in range(BLOCK, ITERS):
+        outer(k, True)
+    sums = lax.fori_loop(0, 8, lambda g, acc: gram(RIM + g + (rows - 8) * (g // 4), acc), sums)
 
     sums = dict(zip(pairs, sums))
     folded = {p: jnp.sum(s, axis=0, keepdims=True) for p, s in sums.items()}
@@ -441,28 +462,29 @@
         spread = jnp.where(lane8 == 8 * k + sub8, total_k, spread)
     mine = jnp.sum(spread, axis=0, keepdims=True)
 
-    def reduce_over(value, slots, send, recv, me, count, device):
-        slots[me] = value
-        copies = []
-        for k in range(1, count):
-            peer = lax.rem(me + k, count)
-            copy = pltpu.make_async_remote_copy(
-                slots.at[me], slots.at[me], send.at[k - 1], recv.at[me],
-                device_id=device(peer), device_id_type=MESH)
-            copy.start()
-            copies.append(copy)
-        for k in range(1, count):
-            src = lax.rem(me + count - k, count)
-            pltpu.make_async_remote_copy(
-                slots.at[src], slots.at[src], send.at[k - 1], recv.at[src],
-                device_id=device(src), device_id_type=MESH).wait_recv()
-        parts = [slots[k] for k in range(count)]
-        while len(parts) > 1:
-            parts = [sum(parts[i : i + 2][1:], parts[i]) for i in range(0, len(parts), 2)]
-        return parts[0], copies
-
-    value, sent = reduce_over(mine, gx_slots, gxs_send, gxs_recv, gx, nx, lambda p: (p, gy))
-    value, more = reduce_over(value, gy_slots, gys_send, gys_recv, gy, ny, lambda p: (gx, p))
+    me = place * ny + gy
+    gx_slots[me] = mine
+    for a, b in hops:
+        copy = pltpu.make_async_remote_copy(
+            gx_slots.at[me], gx_slots.at[me], gxs_send, gxs_recv,
+            device_id=mate(a, b), device_id_type=MESH)
+        copy.start()
+    rest = pl.ds(0, team - 1)
+    every = pltpu.make_async_remote_copy(
+        gx_slots.at[rest], gx_slots.at[rest], gxs_send, gxs_recv,
+        device_id=(east, gy), device_id_type=MESH)
+    every.wait_recv()
+    parts = [gx_slots[k] for k in range(team)]
+    while len(parts) > 1:
+        parts = [sum(parts[i : i + 2][1:], parts[i]) for i in range(0, len(parts), 2)]
+    gy_slots[core] = parts[0]
+    partner = gx + 1 - 2 * core
+    pair = pltpu.make_async_remote_copy(
+        gy_slots.at[core], gy_slots.at[core], gys_send, gys_recv,
+        device_id=(partner, gy), device_id_type=MESH)
+    pair.start()
+    pair.wait_recv()
+    value = gy_slots[0] + gy_slots[1]
 
     value = jnp.broadcast_to(value, (8, 128))
     picked = [jnp.where(lane8 == 8 * k + sub8, value, 0.0) for k in range(10)]
@@ -506,8 +528,9 @@
 
     go_west.wait_send()
     go_east.wait_send()
-    for copy in sent + more:
-        copy.wait_send()
+    await_sent(to_s + [cor_s] + mid_s, to_n + [cor_n] + mid_n)
+    every.wait_send()
+    pair.wait_send()
 
 
 def unfold(outs, sol, res, sem):
@@ -543,11 +566,10 @@
             pltpu.VMEM((CH, CH), F32),
             pltpu.VMEM((2, CH, 128), F32),
             pltpu.VMEM((2, CH, 128), F32),
-            pltpu.VMEM((nx, 1, 128), F32),
-            pltpu.VMEM((ny, 1, 128), F32),
-            dma((2 * CH + 3,)), dma((2,)), dma((2,)), dma((6,)), dma((6,)),
-            dma((2,)), dma((2,)), dma((4,)), dma((4,)),
-            dma((nx,)), dma((nx,)), dma((ny,)), dma((ny,)),
+            pltpu.VMEM((nx // 2 * ny, 1, 128), F32),
+            pltpu.VMEM((2, 1, 128), F32),
+            dma((2 * CH + 3,)), dma((2,)), dma((2,)), dma((10,)), dma((10,)),
+            dma((2,)), dma((2,)), dma((6,)), dma((6,)), dma, dma, dma, dma,
         ],
         compiler_params=pltpu.CompilerParams(
             collective_id=0, has_side_effects=True, vmem_limit_bytes=48 * 1024 * 1024),

time: 41.2 us -> 41.1 us (level)
  the two profiles are of different devices: /device:TPU:0 before, /device:TPU:1 now
where the time goes in v4:
time: 41.1 us; the launch traced here: 40.9 us
  Pallas kernels  39.2 us (95%)
  loops' own time  0.84 us (2%)
  between operations  0.83 us (2%)
    pallas_call x1, Pallas kernels, fused(): pl.pallas_call(functools.partial(kernel, nx, ny), out_shape=(jax.ShapeDty...  38 us
    pallas_call x1, Pallas kernels, fused(): pl.pallas_call(unfold, out_shape=(field, field), in_specs=[vm], out_specs...  1.23 us
    another operation x1, loops' own time, per_device(): lax.while_loop(lambda state: state[2] > 0.5, again, (sol, res, flag[0, 0]))  0.84 us

profile of v4, /device:TPU:1, one launch (start us, length us, event | category | flops | bytes accessed | tf_op | source)
XLA Modules:
  0.0 40.9 jit_solution(7947490879906400050)
XLA Ops:
  0.6 38.0 %krylov.1 = (f32[2,32,16,256]{3,2,1,0:T(8,128)S(1)}, f32[1,1]{1,0:T(1,128)}) custom-call(f32[16,32,256]{2,1,0:T(8,128)} %forc.1, f32[16,32,256]{2,1,0:T(8,128)} %damp.1, f32[32,256]{1,0:T(8,128)} %wlon.1, f32[32,256]{1,0:T(8,128)} %wlat.1, f32[16,16]{1,0:T(8,128)} %coup_hbm.1), custom_call_target="tpu_custom_call" | custom-call | tf_op jit(solution)/shard_map/krylov/pallas_call | solution.py:553
  38.6 1.2 %unfold.1 = (f32[16,32,256]{2,1,0:T(8,128)}, f32[16,32,256]{2,1,0:T(8,128)}) custom-call(f32[2,32,16,256]{3,2,1,0:T(8,128)S(1)} %get-tuple-element.198.outs), custom_call_target="tpu_custom_call" | custom-call | tf_op jit(solution)/shard_map/unfold/pallas_call | solution.py:579
  39.9 0.8 %while.26 = (f32[16,32,256]{2,1,0:T(8,128)}, f32[16,32,256]{2,1,0:T(8,128)}, f32[]{:T(128)}, f32[16,32,256]{2,1,0:T(8,128)}, f32[16,32,256]{2,1,0:T(8,128)}, /*i...) while((f32[16,32,256]{2,1,0:T(8,128)}, f32[16,32,256]{2,1,0:T(8,128)}, f32[]{:T(128)}, ...), condition=%region_11.12_spmd, body=%region_0.11_spmd | while | flops 65700388 | bytes 64118152 | solution.py:678

commit v5 on v4

--- a/solution.py
+++ b/solution.py
@@ -126,18 +126,18 @@
     has_n, has_s = gy < ny - 1, gy > 0
     no_n, no_s = jnp.logical_not(has_n), jnp.logical_not(has_s)
 
-    core, place = lax.rem(gx, 2), gx // 2
-    half_x = nx // 2
-    team = half_x * ny
-    hops = [(a, b) for a in range(half_x) for b in range(ny) if (a, b) != (0, 0)]
-    hops.sort(key=lambda h: min(h[0], half_x - h[0]) + min(h[1], ny - h[1]))
-
-    def mate(a, b):
-        return (2 * lax.rem(place + a, half_x) + core, lax.rem(gy + b, ny))
+    def reach(count):
+        return sorted(range(1, count), key=lambda k: min(k, count - k))
 
     barrier = pltpu.get_barrier_semaphore()
-    for peer in [(east, gy), (west, gy)] + [mate(a, b) for a, b in hops]:
-        pl.semaphore_signal(barrier, 1, device_id=peer, device_id_type=MESH)
+    line_x = [(lax.rem(gx + k, nx), gy) for k in reach(nx)]
+    line_y = [(gx, lax.rem(gy + k, ny)) for k in reach(ny)]
+
+    def greet(some):
+        for peer in some:
+            pl.semaphore_signal(barrier, 1, device_id=peer, device_id_type=MESH)
+
+    greet(line_x[:2] + line_y[:2])
 
     loads = []
     for c in range(CH):
@@ -151,72 +151,10 @@
     loads.append(pltpu.make_async_copy(coup_hbm, coup, in_sem.at[2 * CH + 2]))
     for copy in loads:
         copy.start()
-
+    greet(line_x[2:] + line_y[2:])
     kxv[...] = row_kx(gy * rows - RIM, total, rows * ny)
     for copy in loads:
         copy.wait()
-
-    pl.semaphore_wait(barrier, team + 1)
-
-    def strip(ref, src, dst, size, chan, sem, peer):
-        return pltpu.make_async_remote_copy(
-            ref.at[pl.ds(src, size), chan, pl.ds(0, 256)],
-            ref.at[pl.ds(dst, size), chan, pl.ds(0, 256)],
-            lat_send.at[sem], lat_recv.at[sem], device_id=(gx, peer), device_id_type=MESH)
-
-    def breeze(src, dst, sem, peer):
-        return pltpu.make_async_remote_copy(
-            wind.at[:, pl.ds(src, 8), pl.ds(0, 256)], wind.at[:, pl.ds(dst, 8), pl.ds(0, 256)],
-            lat_send.at[sem], lat_recv.at[sem], device_id=(gx, peer), device_id_type=MESH)
-
-    vec, par = pl.ds(0, CH), pl.ds(CH, CH)
-    near_s = [breeze(RIM, top, 0, south), strip(ext, RIM, top, 4, vec, 1, south),
-              strip(ext, RIM, top, 4, par, 2, south)]
-    far_s = [strip(ext, RIM + 4, top + 4, 4, vec, 3, south),
-             strip(ext, RIM + 4, top + 4, 2, par, 4, south)]
-    near_n = [breeze(rows, 0, 5, north), strip(ext, rows + 4, 4, 4, vec, 6, north),
-              strip(ext, rows + 4, 4, 4, par, 7, north)]
-    far_n = [strip(ext, rows, 0, 4, vec, 8, north), strip(ext, rows + 2, 2, 2, par, 9, north)]
-    to_s, to_n = near_s + far_s, near_n + far_n
-
-    def await_strips(from_s, from_n):
-        @pl.when(has_s)
-        def _():
-            for copy in from_s:
-                copy.wait_recv()
-
-        @pl.when(has_n)
-        def _():
-            for copy in from_n:
-                copy.wait_recv()
-
-    def await_sent(gone_s, gone_n):
-        @pl.when(has_s)
-        def _():
-            for copy in gone_s:
-                copy.wait_send()
-
-        @pl.when(has_n)
-        def _():
-            for copy in gone_n:
-                copy.wait_send()
-
-    @pl.when(has_s)
-    def _():
-        for copy in to_s:
-            copy.start()
-
-    @pl.when(has_n)
-    def _():
-        for copy in to_n:
-            copy.start()
-
-    for missing, row, slot in ((no_s, 0, 0), (no_n, top, groups + 1)):
-        @pl.when(missing)
-        def _():
-            ext[row : row + RIM, 0 : 2 * CH, 0:256] = jnp.zeros((RIM, 2 * CH, 256), F32)
-            wind[:, row : row + RIM, 0:256] = jnp.zeros((2, RIM, 256), F32)
-            lon[:, slot] = jnp.zeros((2, 40, 128), F32)
 
     def turn(value, by):
         by = by % 128
@@ -238,6 +176,8 @@
             b = turn(wind[1, at, cut], 16 + shift)
             pack[side, g, 2 * CH :, :] = jnp.where(lane8 < 16, a, b)
 
+    pl.semaphore_wait(barrier, nx + ny - 2)
+
     go_west = pltpu.make_async_remote_copy(
         pack.at[0], lon.at[0, pl.ds(1, groups)], lon_send.at[0], lon_recv.at[0],
         device_id=(west, gy), device_id_type=MESH)
@@ -247,22 +187,65 @@
     go_west.start()
     go_east.start()
 
-    go_west.wait_recv()
-    go_east.wait_recv()
-    cor_s = pltpu.make_async_remote_copy(
-        lon.at[:, 1], lon.at[:, groups + 1], cor_send.at[0], cor_recv.at[0],
-        device_id=(gx, south), device_id_type=MESH)
-    cor_n = pltpu.make_async_remote_copy(
-        lon.at[:, groups], lon.at[:, 0], cor_send.at[1], cor_recv.at[1],
-        device_id=(gx, north), device_id_type=MESH)
+    def strip(ref, src, dst, size, chan, sem, peer):
+        return pltpu.make_async_remote_copy(
+            ref.at[pl.ds(src, size), chan, pl.ds(0, 256)],
+            ref.at[pl.ds(dst, size), chan, pl.ds(0, 256)],
+            lat_send.at[sem], lat_recv.at[sem], device_id=(gx, peer), device_id_type=MESH)
+
+    def breeze(src, dst, sem, peer):
+        return pltpu.make_async_remote_copy(
+            wind.at[:, pl.ds(src, 8), pl.ds(0, 256)], wind.at[:, pl.ds(dst, 8), pl.ds(0, 256)],
+            lat_send.at[sem], lat_recv.at[sem], device_id=(gx, peer), device_id_type=MESH)
+
+    vec, par = pl.ds(0, CH), pl.ds(CH, CH)
+    near_s = [breeze(RIM, top, 0, south), strip(ext, RIM, top, 4, vec, 1, south),
+              strip(ext, RIM, top, 4, par, 2, south)]
+    far_s = [strip(ext, RIM + 4, top + 4, 4, vec, 3, south),
+             strip(ext, RIM + 4, top + 4, 2, par, 4, south)]
+    near_n = [breeze(rows, 0, 5, north), strip(ext, rows + 4, 4, 4, vec, 6, north),
+              strip(ext, rows + 4, 4, 4, par, 7, north)]
+    far_n = [strip(ext, rows, 0, 4, vec, 8, north), strip(ext, rows + 2, 2, 2, par, 9, north)]
+    to_s, to_n = near_s + far_s, near_n + far_n
+
+    def await_strips(from_s, from_n):
+        @pl.when(has_s)
+        def _():
+            for copy in from_s:
+                copy.wait_recv()
+
+        @pl.when(has_n)
+        def _():
+            for copy in from_n:
+                copy.wait_recv()
+
+    def await_sent(gone_s, gone_n):
+        @pl.when(has_s)
+        def _():
+            for copy in gone_s:
+                copy.wait_send()
+
+        @pl.when(has_n)
+        def _():
+            for copy in gone_n:
+                copy.wait_send()
 
     @pl.when(has_s)
     def _():
-        cor_s.start()
+        for copy in to_s:
+            copy.start()
 
     @pl.when(has_n)
     def _():
-        cor_n.start()
+        for copy in to_n:
+            copy.start()
+
+    for missing, row, slot in ((no_s, 0, 0), (no_n, top, groups + 1)):
+        @pl.when(missing)
+        def _():
+            ext[row : row + RIM, 0 : 2 * CH, 0:256] = jnp.zeros((RIM, 2 * CH, 256), F32)
+            wind[:, row : row + RIM, 0:256] = jnp.zeros((2, RIM, 256), F32)
+            lon[:, slot] = jnp.zeros((2, 40, 128), F32)
 
     two = 2.0 / HALF
     kind = lax.broadcasted_iota(jnp.int32, (8, 128), 0)
@@ -287,11 +270,11 @@
             wind[n, at, 256:384] = merge(
                 turn(lon[0, g, 2 * CH :, :], -16 * n), turn(lon[1, g, 2 * CH :, :], 112 - 16 * n))
 
-    def prepare(g, some=range(8)):
+    def prepare(g, some=range(8), tiles=range(3)):
         at = pl.ds(pl.multiple_of(8 * g, 8), 8)
         kx8 = kxv[at, :]
         in8 = jnp.where(kx8 > 0.0, 1.0, 0.0)
-        for t in range(3):
+        for t in tiles:
             cut = pl.ds(128 * t, 128)
             lon8, lat8 = wind[0, at, cut], wind[1, at, cut]
             for j in some:
@@ -304,8 +287,29 @@
 
     @pl.loop(1, groups + 1)
     def _(g):
+        prepare(g, tiles=range(2))
+
+    go_west.wait_recv()
+    go_east.wait_recv()
+    cor_s = pltpu.make_async_remote_copy(
+        lon.at[:, 1], lon.at[:, groups + 1], cor_send.at[0], cor_recv.at[0],
+        device_id=(gx, south), device_id_type=MESH)
+    cor_n = pltpu.make_async_remote_copy(
+        lon.at[:, groups], lon.at[:, 0], cor_send.at[1], cor_recv.at[1],
+        device_id=(gx, north), device_id_type=MESH)
+
+    @pl.when(has_s)
+    def _():
+        cor_s.start()
+
+    @pl.when(has_n)
+    def _():
+        cor_n.start()
+
+    @pl.loop(1, groups + 1)
+    def _(g):
         third(g)
-        prepare(g)
+        prepare(g, tiles=(2,))
 
     cm = coup[...] * (0.25 * two)
     cm = jnp.concatenate([jnp.concatenate([cm] * 4, axis=1)] * 4, axis=0)
@@ -462,30 +466,24 @@
         spread = jnp.where(lane8 == 8 * k + sub8, total_k, spread)
     mine = jnp.sum(spread, axis=0, keepdims=True)
 
-    me = place * ny + gy
-    gx_slots[me] = mine
-    for a, b in hops:
-        copy = pltpu.make_async_remote_copy(
-            gx_slots.at[me], gx_slots.at[me], gxs_send, gxs_recv,
-            device_id=mate(a, b), device_id_type=MESH)
-        copy.start()
-    rest = pl.ds(0, team - 1)
-    every = pltpu.make_async_remote_copy(
-        gx_slots.at[rest], gx_slots.at[rest], gxs_send, gxs_recv,
-        device_id=(east, gy), device_id_type=MESH)
-    every.wait_recv()
-    parts = [gx_slots[k] for k in range(team)]
-    while len(parts) > 1:
-        parts = [sum(parts[i : i + 2][1:], parts[i]) for i in range(0, len(parts), 2)]
-    gy_slots[core] = parts[0]
-    partner = gx + 1 - 2 * core
-    pair = pltpu.make_async_remote_copy(
-        gy_slots.at[core], gy_slots.at[core], gys_send, gys_recv,
-        device_id=(partner, gy), device_id_type=MESH)
-    pair.start()
-    pair.wait_recv()
-    value = gy_slots[0] + gy_slots[1]
-
+    def reduce_over(value, slots, send, recv, me, count, device):
+        slots[me] = value
+        for k in reversed(reach(count)):
+            pltpu.make_async_remote_copy(
+                slots.at[me], slots.at[me], send, recv,
+                device_id=device(lax.rem(me + k, count)), device_id_type=MESH).start()
+        rest = slots.at[pl.ds(0, count - 1)]
+        every = pltpu.make_async_remote_copy(
+            rest, rest, send, recv,
+            device_id=device(lax.rem(me + 1, count)), device_id_type=MESH)
+        every.wait_recv()
+        parts = [slots[k] for k in range(count)]
+        while len(parts) > 1:
+            parts = [sum(parts[i : i + 2][1:], parts[i]) for i in range(0, len(parts), 2)]
+        return parts[0], every
+
+    value, one_way = reduce_over(mine, gx_slots, gxs_send, gxs_recv, gx, nx, lambda p: (p, gy))
+    value, other_way = reduce_over(value, gy_slots, gys_send, gys_recv, gy, ny, lambda p: (gx, p))
     value = jnp.broadcast_to(value, (8, 128))
     picked = [jnp.where(lane8 == 8 * k + sub8, value, 0.0) for k in range(10)]
     upper = [jnp.broadcast_to(jnp.sum(p, axis=1, keepdims=True), (8, 128)) for p in picked]
@@ -529,8 +527,8 @@
     go_west.wait_send()
     go_east.wait_send()
     await_sent(to_s + [cor_s] + mid_s, to_n + [cor_n] + mid_n)
-    every.wait_send()
-    pair.wait_send()
+    one_way.wait_send()
+    other_way.wait_send()
 
 
 def unfold(outs, sol, res, sem):
@@ -566,8 +564,8 @@
             pltpu.VMEM((CH, CH), F32),
             pltpu.VMEM((2, CH, 128), F32),
             pltpu.VMEM((2, CH, 128), F32),
-            pltpu.VMEM((nx // 2 * ny, 1, 128), F32),
-            pltpu.VMEM((2, 1, 128), F32),
+            pltpu.VMEM((nx, 1, 128), F32),
+            pltpu.VMEM((ny, 1, 128), F32),
             dma((2 * CH + 3,)), dma((2,)), dma((2,)), dma((10,)), dma((10,)),
             dma((2,)), dma((2,)), dma((6,)), dma((6,)), dma, dma, dma, dma,
         ],

time: 41.1 us -> 39.8 us (0.968)
  the two profiles are of different devices: /device:TPU:1 before, /device:TPU:0 now
where the time goes in v5:
time: 39.8 us; the launch traced here: 39.6 us
  Pallas kernels  37.9 us (95%)
  loops' own time  0.84 us (2%)
  between operations  0.83 us (2%)
    pallas_call x1, Pallas kernels, fused(): pl.pallas_call(functools.partial(kernel, nx, ny), out_shape=(jax.ShapeDty...  36.7 us
    pallas_call x1, Pallas kernels, fused(): pl.pallas_call(unfold, out_shape=(field, field), in_specs=[vm], out_specs...  1.23 us
    another operation x1, loops' own time, per_device(): lax.while_loop(lambda state: state[2] > 0.5, again, (sol, res, flag[0, 0]))  0.84 us

profile of v5, /device:TPU:0, one launch (start us, length us, event | category | flops | bytes accessed | tf_op | source)
XLA Modules:
  0.0 39.6 jit_solution(17855603972684668132)
XLA Ops:
  0.6 36.7 %krylov.1 = (f32[2,32,16,256]{3,2,1,0:T(8,128)S(1)}, f32[1,1]{1,0:T(1,128)}) custom-call(f32[16,32,256]{2,1,0:T(8,128)} %forc.1, f32[16,32,256]{2,1,0:T(8,128)} %damp.1, f32[32,256]{1,0:T(8,128)} %wlon.1, f32[32,256]{1,0:T(8,128)} %wlat.1, f32[16,16]{1,0:T(8,128)} %coup_hbm.1), custom_call_target="tpu_custom_call" | custom-call | tf_op jit(solution)/shard_map/krylov/pallas_call | solution.py:551
  37.3 1.2 %unfold.1 = (f32[16,32,256]{2,1,0:T(8,128)}, f32[16,32,256]{2,1,0:T(8,128)}) custom-call(f32[2,32,16,256]{3,2,1,0:T(8,128)S(1)} %get-tuple-element.198.outs), custom_call_target="tpu_custom_call" | custom-call | tf_op jit(solution)/shard_map/unfold/pallas_call | solution.py:577
  38.6 0.8 %while.26 = (f32[16,32,256]{2,1,0:T(8,128)}, f32[16,32,256]{2,1,0:T(8,128)}, f32[]{:T(128)}, f32[16,32,256]{2,1,0:T(8,128)}, f32[16,32,256]{2,1,0:T(8,128)}, /*i...) while((f32[16,32,256]{2,1,0:T(8,128)}, f32[16,32,256]{2,1,0:T(8,128)}, f32[]{:T(128)}, ...), condition=%region_11.12_spmd, body=%region_0.11_spmd | while | flops 65700388 | bytes 64118152 | solution.py:676

commit v6 on v5

--- a/solution.py
+++ b/solution.py
@@ -162,8 +162,7 @@
 
     lane32, lane8 = lanes((2 * CH, 128)), lanes((8, 128))
 
-    @pl.loop(0, groups)
-    def _(g):
+    for g in range(groups):
         for side in range(2):
             shift, cut = (0, pl.ds(0, 128)) if side == 0 else (16, pl.ds(128, 128))
             out = jnp.zeros((2 * CH, 128), F32)
@@ -171,7 +170,7 @@
                 here = (lane32 >= 16 * j) & (lane32 < 16 * j + 16)
                 out = jnp.where(here, turn(ext[RIM + 8 * g + j, :, cut], 16 * j + shift), out)
             pack[side, g, 0 : 2 * CH, :] = out
-            at = pl.ds(pl.multiple_of(RIM + 8 * g, 8), 8)
+            at = pl.ds(RIM + 8 * g, 8)
             a = turn(wind[0, at, cut], shift)
             b = turn(wind[1, at, cut], 16 + shift)
             pack[side, g, 2 * CH :, :] = jnp.where(lane8 < 16, a, b)
@@ -306,8 +305,7 @@
     def _():
         cor_n.start()
 
-    @pl.loop(1, groups + 1)
-    def _(g):
+    for g in range(1, groups + 1):
         third(g)
         prepare(g, tiles=(2,))
 
@@ -325,18 +323,20 @@
 
     lane4 = lanes((4, CH, 128))
 
-    def couple(src, r0):
-        mids = [src[pl.ds(r0, 4), :, 128 * t : 128 * t + 128] for t in range(3)]
+    def couple(src, r0, tiles):
+        mids = [src[pl.ds(r0, 4), :, 128 * t : 128 * t + 128] for t in range(tiles)]
         flat = jnp.concatenate([m.reshape(64, 128) for m in mids], axis=1)
         hi = flat.astype(jnp.bfloat16)
         lo = (flat - hi.astype(F32)).astype(jnp.bfloat16)
         return jnp.dot(weights, jnp.concatenate([hi, lo, hi], axis=0), preferred_element_type=F32)
 
-    def stencil(k, r0, mixed):
+    def stencil(k, r0):
         src, dst = power(k), power(k + 1)
+        tiles = 3 if k + 1 < ITERS else 2
+        mixed = couple(src, r0, tiles)
         prev = power(k - 1) if k % BLOCK else None
         mids = [src[pl.ds(r0, 4), :, 128 * t : 128 * t + 128] for t in range(3)]
-        for t in range(3):
+        for t in range(tiles):
             cut = pl.ds(128 * t, 128)
             mid, nxt, prv = mids[t], mids[(t + 1) % 3], mids[(t + 2) % 3]
             e1 = pltpu.roll(jnp.where(lane4 < 1, nxt, mid), 127, 2)
@@ -359,12 +359,12 @@
     def inner(k):
         m = k % BLOCK + 1
         for r0 in range(RIM + 2 * m, top - 2 * m, 4):
-            stencil(k, r0, couple(power(k), r0))
+            stencil(k, r0)
 
     def outer(k, far):
         m = k % BLOCK + 1
         for r0 in ((2 * m, top - 2 * m + 4) if far else (2 * m + 4, top - 2 * m)):
-            stencil(k, r0, couple(power(k), r0))
+            stencil(k, r0)
 
     for k in range(BLOCK):
         inner(k)
@@ -510,7 +510,7 @@
     qs = [q0[k : k + 1, :] for k in range(8)]
     ds = [left0[k : k + 1, :] for k in range(9)]
 
-    @pl.loop(0, rows)
+    @pl.loop(0, rows, unroll=4)
     def _(r):
         for t in range(2):
             cut = pl.ds(128 * t, 128)

time: 39.8 us -> 39.4 us (0.990)
  no operation moved by 1% of the time
where the time goes in v6:
time: 39.4 us; the launch traced here: 39.2 us
  Pallas kernels  37.6 us (95%)
  between operations  0.81 us (2%)
  loops' own time  0.8 us (2%)
    pallas_call x1, Pallas kernels, fused(): pl.pallas_call(functools.partial(kernel, nx, ny), out_shape=(jax.ShapeDty...  36.3 us
    pallas_call x1, Pallas kernels, fused(): pl.pallas_call(unfold, out_shape=(field, field), in_specs=[vm], out_specs...  1.23 us
    another operation x1, loops' own time, per_device(): lax.while_loop(lambda state: state[2] > 0.5, again, (sol, res, flag[0, 0]))  0.8 us

profile of v6, /device:TPU:0, one launch (start us, length us, event | category | flops | bytes accessed | tf_op | source)
XLA Modules:
  0.0 39.2 jit_solution(3357465274259867609)
XLA Ops:
  0.6 36.3 %krylov.1 = (f32[2,32,16,256]{3,2,1,0:T(8,128)S(1)}, f32[1,1]{1,0:T(1,128)}) custom-call(f32[16,32,256]{2,1,0:T(8,128)} %forc.1, f32[16,32,256]{2,1,0:T(8,128)} %damp.1, f32[32,256]{1,0:T(8,128)} %wlon.1, f32[32,256]{1,0:T(8,128)} %wlat.1, f32[16,16]{1,0:T(8,128)} %coup_hbm.1), custom_call_target="tpu_custom_call" | custom-call | tf_op jit(solution)/shard_map/krylov/pallas_call | solution.py:551
  37.0 1.2 %unfold.1 = (f32[16,32,256]{2,1,0:T(8,128)}, f32[16,32,256]{2,1,0:T(8,128)}) custom-call(f32[2,32,16,256]{3,2,1,0:T(8,128)S(1)} %get-tuple-element.198.outs), custom_call_target="tpu_custom_call" | custom-call | tf_op jit(solution)/shard_map/unfold/pallas_call | solution.py:577
  38.2 0.8 %while.26 = (f32[16,32,256]{2,1,0:T(8,128)}, f32[16,32,256]{2,1,0:T(8,128)}, f32[]{:T(128)}, f32[16,32,256]{2,1,0:T(8,128)}, f32[16,32,256]{2,1,0:T(8,128)}, /*i...) while((f32[16,32,256]{2,1,0:T(8,128)}, f32[16,32,256]{2,1,0:T(8,128)}, f32[]{:T(128)}, ...), condition=%region_11.12_spmd, body=%region_0.11_spmd | while | flops 65700388 | bytes 64118152 | solution.py:676
